TPU v7x, 32 devices: a whole 2x2x4 slice. The times are simulated.
32 devices in a mesh: grp: 2 (over x), row: 8 (over z, core), col: 2 (over y).
Axes of the slice: x: 2, y: 2, z: 4, core: 2. Of those that a mesh axis runs over, the one named last changes fastest.
Arguments:
- vectors: float32 [64, 128, 512], P('grp', 'row', 'col'), may hold values from -6 to 6
- disorder: float32 [128, 512], P('row', 'col'), may hold values from -1.5 to 1.5
Outputs:
- cheb_prev: float32 [64, 128, 512], P('grp', 'row', 'col')
- cheb_last: float32 [64, 128, 512], P('grp', 'row', 'col')
- moments: float32 [17], replicated
All inputs are finite; a program needn't handle non-finite values.
Results may differ from a plain program's by a relative error of at most 0.0001.
Values sent between devices are 32-bit elements; how exact they have to be, the bound alone decides.
No kernel may reach another device: no remote copies, remote signals or barrier semaphores. Data moves between devices by JAX's collectives and lax.ppermute only.
A program may use at most 64 MiB of HBM per device.

v0:
```python
import jax
import jax.numpy as jnp
from jax import lax
from jax.sharding import PartitionSpec as P

STEPS = 8


SCALE = 4.6


def extended(block, sides, width):
    for axis, dim in sides:
        count = lax.axis_size(axis)
        forward = [(i, i + 1) for i in range(count - 1)]
        forward.append((count - 1, 0))
        backward = [(target, source) for source, target in forward]
        low = lax.ppermute(
            lax.slice_in_dim(block, block.shape[dim] - width, None, axis=dim), axis, forward
        )
        high = lax.ppermute(lax.slice_in_dim(block, 0, width, axis=dim), axis, backward)
        block = jnp.concatenate([low, block, high], axis=dim)
    return block


def inner_hop(field, dis_part, even_part):
    left = field[:, 1:-1, :-2]
    right = field[:, 1:-1, 2:]
    below = field[:, 2:, 1:-1]
    above = field[:, :-2, 1:-1]
    center = field[:, 1:-1, 1:-1]
    vertical = jnp.where(even_part, below, above)
    return (dis_part * center - (left + right + vertical)) / SCALE


def body(vectors, disorder):
    vecs, rows_here, cols_here = vectors.shape
    count = float(
        vecs
        * lax.axis_size("grp")
        * rows_here
        * lax.axis_size("row")
        * cols_here
        * lax.axis_size("col")
    )
    margin = 4
    dis_pad = extended(disorder, (("row", 0), ("col", 1)), margin)
    rows = lax.broadcasted_iota(jnp.int32, dis_pad.shape, 0)
    cols = lax.broadcasted_iota(jnp.int32, dis_pad.shape, 1)
    even_pad = (rows + cols) % 2 == 0

    def advance(field):
        extra = (field.shape[1] - rows_here) // 2
        start = margin - extra
        stop_r = start + field.shape[1] - 1
        stop_c = start + field.shape[2] - 1
        dis_part = dis_pad[start + 1 : stop_r, start + 1 : stop_c]
        even_part = even_pad[start + 1 : stop_r, start + 1 : stop_c][None]
        return inner_hop(field, dis_part, even_part)

    def interior(field):
        extra = (field.shape[1] - rows_here) // 2
        return field[:, extra : extra + rows_here, extra : extra + cols_here]

    older = vectors
    newer = vectors
    squares = [jnp.sum(vectors * vectors)]
    crosses = []
    for rounds in range(STEPS // margin):
        padded_old, padded_new = (
            extended(older, (("row", 1), ("col", 2)), margin),
            extended(newer, (("row", 1), ("col", 2)), margin),
        )
        for inner in range(margin):
            if rounds == 0 and inner == 0:
                latest = advance(padded_new)
            else:
                latest = 2.0 * advance(padded_new) - padded_old[:, 1:-1, 1:-1]
            padded_old = padded_new[:, 1:-1, 1:-1]
            padded_new = latest
            kept_new = interior(padded_new)
            kept_old = interior(padded_old)
            squares.append(jnp.sum(kept_new * kept_new))
            crosses.append(jnp.sum(kept_new * kept_old))
        older, newer = (padded_old, padded_new)
    total_squares = [lax.psum(squares[0], ("grp", "row", "col"))]
    total_crosses = []
    for index in range(STEPS):
        pair = lax.psum((squares[index + 1], crosses[index]), ("grp", "row", "col"))
        total_squares.append(pair[0])
        total_crosses.append(pair[1])
    total_squares = jnp.stack(total_squares)
    total_crosses = jnp.stack(total_crosses)
    total_squares = total_squares / count
    total_crosses = total_crosses / count
    first = total_squares[0]
    second = total_crosses[0]
    values = [first, second]
    for index in range(1, STEPS + 1):
        values.append(2.0 * total_squares[index] - first)
        if index < STEPS:
            values.append(2.0 * total_crosses[index] - second)
    return (older, newer, jnp.stack(values))


def solution(mesh):
    placed = (P("grp", "row", "col"), P("row", "col"))
    return jax.shard_map(
        body,
        mesh=mesh,
        in_specs=placed,
        out_specs=(P("grp", "row", "col"), P("grp", "row", "col"), P()),
        check_vma=False,
    )
```

profile of v0, /device:TPU:0, one launch (start us, length us, event | category | flops | bytes accessed | tf_op | source)
XLA Modules:
  0.0 162.1 jit_solution(18027950216888657291)
XLA Ops:
  1.8 4.0 %collective-permute-start.1 = (f32[4,256]{1,0:T(4,128)S(1)}, f32[4,256]{1,0:T(4,128)S(1)}, u32[]{:S(2)}, u32[]{:S(2)}) collective-permute-start(f32[4,256]{1,0:T(4,128)S(1)} %get-tuple-element.64), channel_id=1, source_target_pairs={{2,0},{4,2},{6,4},{8,6},{10,8},{12,10},{14,12},{0,14},{3,1},{5,3},... | collective-permute-start | bytes 12296 | tf_op jit(solution)/shard_map/ppermute | solution.py:21
  5.9 1.1 fusion.39
  7.0 3.5 %collective-permute-start.5 = (f32[32,4,256]{2,1,0:T(4,128)S(1)}, f32[32,4,256]{2,1,0:T(4,128)S(1)}, u32[]{:S(2)}, u32[]{:S(2)}) collective-permute-start(f32[32,4,256]{2,1,0:T(4,128)S(1)} %get-tuple-element.60), channel_id=1, source_target_pairs={{2,0},{4,2},{6,4},{8,6},{10,8},{12,10},{14,12},{0,14},{3,1},{5,3},... | collective-permute-start | bytes 393224 | tf_op jit(solution)/shard_map/ppermute | solution.py:21
  10.9 0.7 pad_maximum_fusion.10
  11.7 2.0 %collective-permute-start.2 = (f32[24,4]{1,0:T(8,128)S(1)}, f32[24,4]{1,0:T(8,128)S(1)}, u32[]{:S(2)}, u32[]{:S(2)}) collective-permute-start(f32[24,4]{1,0:T(8,128)S(1)} %get-tuple-element.61), channel_id=1, source_target_pairs={{0,1},{1,0},{2,3},{3,2},{4,5},{5,4},{6,7},{7,6},{8,9},{9,8},{10,11... | collective-permute-start | bytes 1160 | tf_op jit(solution)/shard_map/ppermute | solution.py:18
  13.8 1.2 pad_maximum_fusion.6
  15.2 2.6 %collective-permute-start.6 = (f32[32,24,4]{2,1,0:T(8,128)S(1)}, f32[32,24,4]{2,1,0:T(8,128)S(1)}, u32[]{:S(2)}, u32[]{:S(2)}) collective-permute-start(f32[32,24,4]{2,1,0:T(8,128)S(1)} %get-tuple-element.55), channel_id=1, source_target_pairs={{0,1},{1,0},{2,3},{3,2},{4,5},{5,4},{6,7},{7,6},{8,9},{9,8},{10,11... | collective-permute-start | bytes 36872 | tf_op jit(solution)/shard_map/ppermute | solution.py:18
  18.2 9.5 %collective-permute-done.6 = f32[32,24,4]{2,1,0:T(8,128)S(1)} collective-permute-done((f32[32,24,4]{2,1,0:T(8,128)S(1)}, f32[32,24,4]{2,1,0:T(8,128)S(1)}, u32[]{:S(2)}, u32[]{:S(2)}) %collective-permute-start.6) | collective-permute-done | bytes 12320 | tf_op jit(solution)/shard_map/ppermute | solution.py:18
  27.7 6.4 %collective-permute-done.7 = f32[32,24,4]{2,1,0:T(8,128)S(1)} collective-permute-done((f32[32,24,4]{2,1,0:T(8,128)S(1)}, f32[32,24,4]{2,1,0:T(8,128)S(1)}, u32[]{:S(2)}, u32[]{:S(2)}) %collective-permute-start.7) | collective-permute-done | bytes 12320 | tf_op jit(solution)/shard_map/ppermute | solution.py:21
  34.8 1.3 fusion.18
  36.1 1.6 slice_subtract_fusion.3
  37.7 1.6 slice_subtract_fusion.2
  39.3 0.7 fusion.34
  40.2 3.5 %collective-permute-start.9 = (f32[32,4,256]{2,1,0:T(4,128)S(1)}, f32[32,4,256]{2,1,0:T(4,128)S(1)}, u32[]{:S(2)}, u32[]{:S(2)}) collective-permute-start(f32[32,4,256]{2,1,0:T(4,128)S(1)} %get-tuple-element.58), channel_id=1, source_target_pairs={{2,0},{4,2},{6,4},{8,6},{10,8},{12,10},{14,12},{0,14},{3,1},{5,3},... | collective-permute-start | bytes 393224 | tf_op jit(solution)/shard_map/ppermute | solution.py:21
  44.0 3.5 %collective-permute-start.13 = (f32[32,4,256]{2,1,0:T(4,128)S(1)}, f32[32,4,256]{2,1,0:T(4,128)S(1)}, u32[]{:S(2)}, u32[]{:S(2)}) collective-permute-start(f32[32,4,256]{2,1,0:T(4,128)S(1)} %get-tuple-element.48), channel_id=1, source_target_pairs={{2,0},{4,2},{6,4},{8,6},{10,8},{12,10},{14,12},{0,14},{3,1},{5,3},... | collective-permute-start | bytes 393224 | tf_op jit(solution)/shard_map/ppermute | solution.py:21
  48.4 1.8 %collective-permute-start.11 = (f32[32,24,4]{2,1,0:T(8,128)S(1)}, f32[32,24,4]{2,1,0:T(8,128)S(1)}, u32[]{:S(2)}, u32[]{:S(2)}) collective-permute-start(f32[32,24,4]{2,1,0:T(8,128)S(1)} %get-tuple-element.54), channel_id=1, source_target_pairs={{1,0},{0,1},{3,2},{2,3},{5,4},{4,5},{7,6},{6,7},{9,8},{8,9},{11,10... | collective-permute-start | bytes 36872 | tf_op jit(solution)/shard_map/ppermute | solution.py:21
  50.6 0.8 collective-permute-start.14
  51.3 1.3 collective-permute-start.15
  52.7 7.5 %collective-permute-done.10 = f32[32,24,4]{2,1,0:T(8,128)S(1)} collective-permute-done((f32[32,24,4]{2,1,0:T(8,128)S(1)}, f32[32,24,4]{2,1,0:T(8,128)S(1)}, u32[]{:S(2)}, u32[]{:S(2)}) %collective-permute-start.10) | collective-permute-done | bytes 12320 | tf_op jit(solution)/shard_map/ppermute | solution.py:18
  60.1 8.4 %collective-permute-done.11 = f32[32,24,4]{2,1,0:T(8,128)S(1)} collective-permute-done((f32[32,24,4]{2,1,0:T(8,128)S(1)}, f32[32,24,4]{2,1,0:T(8,128)S(1)}, u32[]{:S(2)}, u32[]{:S(2)}) %collective-permute-start.11) | collective-permute-done | bytes 12320 | tf_op jit(solution)/shard_map/ppermute | solution.py:21
  68.6 0.7 pad_maximum_fusion.5
  69.3 7.7 %collective-permute-done.14 = f32[32,24,4]{2,1,0:T(8,128)S(1)} collective-permute-done((f32[32,24,4]{2,1,0:T(8,128)S(1)}, f32[32,24,4]{2,1,0:T(8,128)S(1)}, u32[]{:S(2)}, u32[]{:S(2)}) %collective-permute-start.14) | collective-permute-done | bytes 12320 | tf_op jit(solution)/shard_map/ppermute | solution.py:18
  77.0 4.4 %collective-permute-done.15 = f32[32,24,4]{2,1,0:T(8,128)S(1)} collective-permute-done((f32[32,24,4]{2,1,0:T(8,128)S(1)}, f32[32,24,4]{2,1,0:T(8,128)S(1)}, u32[]{:S(2)}, u32[]{:S(2)}) %collective-permute-start.15) | collective-permute-done | bytes 12320 | tf_op jit(solution)/shard_map/ppermute | solution.py:21
  81.4 2.1 %fusion.6 = f32[32,22,262]{2,1,0:T(8,128)S(1)} fusion(f32[32,24,4]{2,1,0:T(8,128)S(1)} %collective-permute-done.15, f32[32,24,4]{2,1,0:T(8,128)S(1)} %collective-permute-done.14, f32[32,4,256]{2,1,0:T(4,128)S(1)} %collective-permute-done.13, f32[32,16,256]{2,1,0:T(8,128)S(1)} %get-tuple-element.49, f32[32,4,256]{2,1,0:T(4,128)S(1)} %collective-permute-done.12, ...), kind=kLoop, calls=%fused_computation.15 | loop fusion | flops 2028928 | bytes 5266580 | tf_op jit(solution)/shard_map/sub | solution.py:78
  83.5 1.6 slice_subtract_fusion.1
  85.1 1.6 slice_subtract_fusion
  86.7 1.3 multiply_reduce_fusion.8
  88.1 1.6 %multiply_reduce_fusion.1 = (f32[]{:T(128)}, f32[]{:T(128)}, f32[]{:T(128)}, f32[]{:T(128)}, f32[]{:T(128)}, /*index=5*/f32[]{:T(128)}, f32[]{:T(128)}, f32[]{:T...) fusion(f32[32,16,256]{2,1,0:T(8,128)S(1)} %get-tuple-element.46, ...), kind=kLoop, calls=%fused_computation.63 | loop fusion | flops 4194288 | bytes 4718656 | tf_op jit(solution)/shard_map/reduce_sum | solution.py:84
  89.7 40.1 %all-reduce = (f32[1]{0:T(128)}, f32[1]{0:T(128)}, f32[1]{0:T(128)}, f32[1]{0:T(128)}, f32[1]{0:T(128)}, /*index=5*/f32[1]{0:T(128)}, f32[1]{0:T(128)}, f32[1]{0...) all-reduce(f32[1]{0:T(128)} %bitcast, f32[1]{0:T(128)} %bitcast.1, ...), channel_id=1, replica_groups=mesh['grp'=2,'row'=8,'col'=2] {'grp','row','col'}, use_global_device_ids=true, to_apply=%region_1.2 | all-reduce | flops 17 | bytes 136 | tf_op jit(solution)/shard_map/psum | solution.py:86
  129.8 5.7 %stack.84 = f32[9]{0:T(128)S(1)} concatenate(f32[1]{0:T(128)} %get-tuple-element.27, f32[1]{0:T(128)} %get-tuple-element.28, f32[1]{0:T(128)} %get-tuple-element.29, f32[1]{0:T(128)} %get-tuple-element.30, f32[1]{0:T(128)} %get-tuple-element.31, f32[1]{0:T(128)} %get-tuple-element.32, f32[1]{0:T(128)} %get-tuple-element.33, f32[1]{0:T(128)} %get-tuple-element.34, f32[1]{0:T(128)} %get-tuple-element.35), dimensions={0} | concatenate | bytes 72 | tf_op jit(solution)/shard_map/stack | solution.py:92
  135.5 5.2 %stack.93 = f32[8]{0:T(128)S(1)} concatenate(f32[1]{0:T(128)} %get-tuple-element.36, f32[1]{0:T(128)} %get-tuple-element.37, f32[1]{0:T(128)} %get-tuple-element.38, f32[1]{0:T(128)} %get-tuple-element.39, f32[1]{0:T(128)} %get-tuple-element.40, f32[1]{0:T(128)} %get-tuple-element.41, f32[1]{0:T(128)} %get-tuple-element.42, f32[1]{0:T(128)} %get-tuple-element.43), dimensions={0} | concatenate | bytes 64 | tf_op jit(solution)/shard_map/stack | solution.py:93
  160.2 1.9 %stack.94 = f32[17]{0:T(128)} concatenate(f32[1]{0:T(128)} %get-tuple-element.73, f32[1]{0:T(128)} %get-tuple-element.82, f32[1]{0:T(128)S(6)} %sub.120, f32[1]{0:T(128)S(6)} %sub.121, f32[1]{0:T(128)S(6)} %sub.122, f32[1]{0:T(128)S(6)} %sub.123, f32[1]{0:T(128)S(6)} %sub.124, f32[1]{0:T(128)S(6)} %sub.125, f32[1]{0:T(128)S(6)} %sub.126, f32[1]{0:T(128)S(6)} %sub.127, ...), dimensions={0} | concatenate | bytes 136 | tf_op jit(solution)/shard_map/stack | solution.py:103
  (47 shorter events, 5.4 us)
Async XLA Ops:
  1.4 9.6 %collective-permute-start = (f32[4,256]{1,0:T(4,128)S(1)}, f32[4,256]{1,0:T(4,128)S(1)}, u32[]{:S(2)}, u32[]{:S(2)}) collective-permute-start(f32[4,256]{1,0:T(4,128)S(1)} %get-tuple-element.63), channel_id=1, source_target_pairs={{0,2},{2,4},{4,6},{6,8},{8,10},{10,12},{12,14},{14,0},{1,3},{3,5},... | collective-permute-start | bytes 12296 | tf_op jit(solution)/shard_map/ppermute | solution.py:18
  1.8 9.1 %collective-permute-start.1 = (f32[4,256]{1,0:T(4,128)S(1)}, f32[4,256]{1,0:T(4,128)S(1)}, u32[]{:S(2)}, u32[]{:S(2)}) collective-permute-start(f32[4,256]{1,0:T(4,128)S(1)} %get-tuple-element.64), channel_id=1, source_target_pairs={{2,0},{4,2},{6,4},{8,6},{10,8},{12,10},{14,12},{0,14},{3,1},{5,3},... | collective-permute-start | bytes 12296 | tf_op jit(solution)/shard_map/ppermute | solution.py:21
  7.0 6.9 %collective-permute-start.4 = (f32[32,4,256]{2,1,0:T(4,128)S(1)}, f32[32,4,256]{2,1,0:T(4,128)S(1)}, u32[]{:S(2)}, u32[]{:S(2)}) collective-permute-start(f32[32,4,256]{2,1,0:T(4,128)S(1)} %get-tuple-element.59), channel_id=1, source_target_pairs={{0,2},{2,4},{4,6},{6,8},{8,10},{10,12},{12,14},{14,0},{1,3},{3,5},... | collective-permute-start | bytes 393224 | tf_op jit(solution)/shard_map/ppermute | solution.py:18
  7.0 6.8 %collective-permute-start.5 = (f32[32,4,256]{2,1,0:T(4,128)S(1)}, f32[32,4,256]{2,1,0:T(4,128)S(1)}, u32[]{:S(2)}, u32[]{:S(2)}) collective-permute-start(f32[32,4,256]{2,1,0:T(4,128)S(1)} %get-tuple-element.60), channel_id=1, source_target_pairs={{2,0},{4,2},{6,4},{8,6},{10,8},{12,10},{14,12},{0,14},{3,1},{5,3},... | collective-permute-start | bytes 393224 | tf_op jit(solution)/shard_map/ppermute | solution.py:21
  11.7 6.1 %collective-permute-start.2 = (f32[24,4]{1,0:T(8,128)S(1)}, f32[24,4]{1,0:T(8,128)S(1)}, u32[]{:S(2)}, u32[]{:S(2)}) collective-permute-start(f32[24,4]{1,0:T(8,128)S(1)} %get-tuple-element.61), channel_id=1, source_target_pairs={{0,1},{1,0},{2,3},{3,2},{4,5},{5,4},{6,7},{7,6},{8,9},{9,8},{10,11... | collective-permute-start | bytes 1160 | tf_op jit(solution)/shard_map/ppermute | solution.py:18
  13.7 4.1 %collective-permute-start.3 = (f32[24,4]{1,0:T(8,128)S(1)}, f32[24,4]{1,0:T(8,128)S(1)}, u32[]{:S(2)}, u32[]{:S(2)}) collective-permute-start(f32[24,4]{1,0:T(8,128)S(1)} %get-tuple-element.62), channel_id=1, source_target_pairs={{1,0},{0,1},{3,2},{2,3},{5,4},{4,5},{7,6},{6,7},{9,8},{8,9},{11,10... | collective-permute-start | bytes 1160 | tf_op jit(solution)/shard_map/ppermute | solution.py:21
  15.0 2.8 %copy-start.3 = (f32[16,256]{1,0:T(8,128)S(1)}, f32[16,256]{1,0:T(8,128)}, u32[]{:S(2)}) copy-start(f32[16,256]{1,0:T(8,128)} %param.3) | copy-start | bytes 49156
  15.0 19.1 %copy-start = (f32[32,16,256]{2,1,0:T(8,128)S(1)}, f32[32,16,256]{2,1,0:T(8,128)}, u32[]{:S(2)}) copy-start(f32[32,16,256]{2,1,0:T(8,128)} %param.2) | copy-start | bytes 1572868
  15.2 12.5 %collective-permute-start.6 = (f32[32,24,4]{2,1,0:T(8,128)S(1)}, f32[32,24,4]{2,1,0:T(8,128)S(1)}, u32[]{:S(2)}, u32[]{:S(2)}) collective-permute-start(f32[32,24,4]{2,1,0:T(8,128)S(1)} %get-tuple-element.55), channel_id=1, source_target_pairs={{0,1},{1,0},{2,3},{3,2},{4,5},{5,4},{6,7},{7,6},{8,9},{9,8},{10,11... | collective-permute-start | bytes 36872 | tf_op jit(solution)/shard_map/ppermute | solution.py:18
  17.7 16.3 %collective-permute-start.7 = (f32[32,24,4]{2,1,0:T(8,128)S(1)}, f32[32,24,4]{2,1,0:T(8,128)S(1)}, u32[]{:S(2)}, u32[]{:S(2)}) collective-permute-start(f32[32,24,4]{2,1,0:T(8,128)S(1)} %get-tuple-element.56), channel_id=1, source_target_pairs={{1,0},{0,1},{3,2},{2,3},{5,4},{4,5},{7,6},{6,7},{9,8},{8,9},{11,10... | collective-permute-start | bytes 36872 | tf_op jit(solution)/shard_map/ppermute | solution.py:21
  40.1 7.6 %collective-permute-start.8 = (f32[32,4,256]{2,1,0:T(4,128)S(1)}, f32[32,4,256]{2,1,0:T(4,128)S(1)}, u32[]{:S(2)}, u32[]{:S(2)}) collective-permute-start(f32[32,4,256]{2,1,0:T(4,128)S(1)} %get-tuple-element.57), channel_id=1, source_target_pairs={{0,2},{2,4},{4,6},{6,8},{8,10},{10,12},{12,14},{14,0},{1,3},{3,5},... | collective-permute-start | bytes 393224 | tf_op jit(solution)/shard_map/ppermute | solution.py:18
  40.2 7.6 %collective-permute-start.9 = (f32[32,4,256]{2,1,0:T(4,128)S(1)}, f32[32,4,256]{2,1,0:T(4,128)S(1)}, u32[]{:S(2)}, u32[]{:S(2)}) collective-permute-start(f32[32,4,256]{2,1,0:T(4,128)S(1)} %get-tuple-element.58), channel_id=1, source_target_pairs={{2,0},{4,2},{6,4},{8,6},{10,8},{12,10},{14,12},{0,14},{3,1},{5,3},... | collective-permute-start | bytes 393224 | tf_op jit(solution)/shard_map/ppermute | solution.py:21
  43.9 6.3 %collective-permute-start.12 = (f32[32,4,256]{2,1,0:T(4,128)S(1)}, f32[32,4,256]{2,1,0:T(4,128)S(1)}, u32[]{:S(2)}, u32[]{:S(2)}) collective-permute-start(f32[32,4,256]{2,1,0:T(4,128)S(1)} %get-tuple-element.47), channel_id=1, source_target_pairs={{0,2},{2,4},{4,6},{6,8},{8,10},{10,12},{12,14},{14,0},{1,3},{3,5},... | collective-permute-start | bytes 393224 | tf_op jit(solution)/shard_map/ppermute | solution.py:18
  44.0 6.3 %collective-permute-start.13 = (f32[32,4,256]{2,1,0:T(4,128)S(1)}, f32[32,4,256]{2,1,0:T(4,128)S(1)}, u32[]{:S(2)}, u32[]{:S(2)}) collective-permute-start(f32[32,4,256]{2,1,0:T(4,128)S(1)} %get-tuple-element.48), channel_id=1, source_target_pairs={{2,0},{4,2},{6,4},{8,6},{10,8},{12,10},{14,12},{0,14},{3,1},{5,3},... | collective-permute-start | bytes 393224 | tf_op jit(solution)/shard_map/ppermute | solution.py:21
  48.1 12.1 %collective-permute-start.10 = (f32[32,24,4]{2,1,0:T(8,128)S(1)}, f32[32,24,4]{2,1,0:T(8,128)S(1)}, u32[]{:S(2)}, u32[]{:S(2)}) collective-permute-start(f32[32,24,4]{2,1,0:T(8,128)S(1)} %get-tuple-element.53), channel_id=1, source_target_pairs={{0,1},{1,0},{2,3},{3,2},{4,5},{5,4},{6,7},{7,6},{8,9},{9,8},{10,11... | collective-permute-start | bytes 36872 | tf_op jit(solution)/shard_map/ppermute | solution.py:18
  48.4 20.2 %collective-permute-start.11 = (f32[32,24,4]{2,1,0:T(8,128)S(1)}, f32[32,24,4]{2,1,0:T(8,128)S(1)}, u32[]{:S(2)}, u32[]{:S(2)}) collective-permute-start(f32[32,24,4]{2,1,0:T(8,128)S(1)} %get-tuple-element.54), channel_id=1, source_target_pairs={{1,0},{0,1},{3,2},{2,3},{5,4},{4,5},{7,6},{6,7},{9,8},{8,9},{11,10... | collective-permute-start | bytes 36872 | tf_op jit(solution)/shard_map/ppermute | solution.py:21
  50.6 26.4 %collective-permute-start.14 = (f32[32,24,4]{2,1,0:T(8,128)S(1)}, f32[32,24,4]{2,1,0:T(8,128)S(1)}, u32[]{:S(2)}, u32[]{:S(2)}) collective-permute-start(f32[32,24,4]{2,1,0:T(8,128)S(1)} %get-tuple-element.51), channel_id=1, source_target_pairs={{0,1},{1,0},{2,3},{3,2},{4,5},{5,4},{6,7},{7,6},{8,9},{9,8},{10,11... | collective-permute-start | bytes 36872 | tf_op jit(solution)/shard_map/ppermute | solution.py:18
  51.3 30.1 %collective-permute-start.15 = (f32[32,24,4]{2,1,0:T(8,128)S(1)}, f32[32,24,4]{2,1,0:T(8,128)S(1)}, u32[]{:S(2)}, u32[]{:S(2)}) collective-permute-start(f32[32,24,4]{2,1,0:T(8,128)S(1)} %get-tuple-element.52), channel_id=1, source_target_pairs={{1,0},{0,1},{3,2},{2,3},{5,4},{4,5},{7,6},{6,7},{9,8},{8,9},{11,10... | collective-permute-start | bytes 36872 | tf_op jit(solution)/shard_map/ppermute | solution.py:21
  88.1 1.7 %copy-start.1 = (f32[32,16,256]{2,1,0:T(8,128)}, f32[32,16,256]{2,1,0:T(8,128)S(1)}, u32[]{:S(2)}) copy-start(f32[32,16,256]{2,1,0:T(8,128)S(1)} %get-tuple-element.45) | copy-start | bytes 1572868
  88.1 1.7 %copy-start.2 = (f32[32,16,256]{2,1,0:T(8,128)}, f32[32,16,256]{2,1,0:T(8,128)S(1)}, u32[]{:S(2)}) copy-start(f32[32,16,256]{2,1,0:T(8,128)S(1)} %get-tuple-element.46) | copy-start | bytes 1572868
where the time goes:
time: 163 us; the launch traced here: 162 us
  waiting for transfers between devices  44.3 us (27%)
  blocking collectives  40.1 us (25%)
  starting transfers between devices  24.2 us (15%)
  between operations  19.6 us (12%)
  other arithmetic  17.3 us (11%)
  local copies, waits for them, and re-layouts  16.7 us (10%)
    psum x1, blocking collectives, body(): total_squares = [lax.psum(squares[0], ('grp', 'row', 'col'))]  40.1 us
    ppermute x8, waiting for transfers between devices, extended(): lax.ppermute(lax.slice_in_dim(block, block.shape[dim] - width, None, axis...  25.1 us
    ppermute x8, waiting for transfers between devices, extended(): lax.ppermute(lax.slice_in_dim(block, 0, width, axis=dim), axis, backward)  19.2 us
    ppermute x8, starting transfers between devices, extended(): lax.ppermute(lax.slice_in_dim(block, 0, width, axis=dim), axis, backward)  17.9 us
    sub x5, other arithmetic, body(): latest = 2.0 * advance(padded_new) - padded_old[:, 1:-1, 1:-1]  8.54 us
    ppermute x8, starting transfers between devices, extended(): lax.ppermute(lax.slice_in_dim(block, block.shape[dim] - width, None, axis...  6.28 us
    another operation x1, local copies, waits for them, and re-layouts, body(): total_squares = jnp.stack(total_squares)  5.71 us
    another operation x1, local copies, waits for them, and re-layouts, body(): total_crosses = jnp.stack(total_crosses)  5.19 us
  transfers between devices with their start and end apart: 16, of which 8 were waited for; matrix products, arithmetic and copies ran while one was open for 3% of the time, Pallas kernels for 0%

commit v1 on v0

v1 whole, which is shorter than its diff:
```python
import functools

import jax
import jax.numpy as jnp
from jax import lax
from jax.experimental import pallas as pl
from jax.experimental.pallas import tpu as pltpu
from jax.sharding import PartitionSpec as P

STEPS = 8
SCALE = 4.6
RIM_R = (STEPS + 1) // 2
RIM_C = STEPS
LANES = 128
AXES = ("grp", "row", "col")

VMEM = pl.BlockSpec(memory_space=pltpu.VMEM)
ANY = pl.BlockSpec(memory_space=pl.ANY)


def pack_kernel(vec, dis, top, mid, bot, sem):
    vecs, rows, _ = vec.shape
    copies = []
    for r in range(rows):
        if r < RIM_R:
            dst = top.at[pl.ds(r * vecs, vecs), :]
        elif r < rows - RIM_R:
            dst = mid.at[pl.ds((r - RIM_R) * vecs, vecs), :]
        else:
            dst = bot.at[pl.ds((r - rows + RIM_R) * vecs, vecs), :]
        copies.append(pltpu.make_async_copy(vec.at[:, r, :], dst, sem.at[r]))
    for copy in copies:
        copy.start()
    top[RIM_R * vecs :, :] = dis[:8, :]
    bot[RIM_R * vecs :, :] = dis[rows - 8 :, :]
    for copy in copies:
        copy.wait()


def row_source(p, rows, vecs, lo, top, mid, bot, hi):
    for ref, count in ((lo, RIM_R), (top, RIM_R), (mid, rows - 2 * RIM_R), (bot, RIM_R), (hi, RIM_R)):
        if p < count:
            return ref, p * vecs
        p -= count


def turn_kernel(rows, vecs, lo, top, mid, bot, hi, dis, field, edges, dis_pad):
    groups = LANES // vecs
    padded = rows + 2 * RIM_R
    depth = padded // groups
    cols = dis.shape[1]
    at = RIM_R * vecs
    dis_pad[...] = jnp.concatenate(
        [lo[at + 8 - RIM_R : at + 8, :], dis[...], hi[at : at + RIM_R, :]], axis=0
    )
    for m in range(depth):
        for c in range(0, cols, LANES):
            parts = []
            for g in range(groups):
                ref, line = row_source(g * depth + m, rows, vecs, lo, top, mid, bot, hi)
                parts.append(ref[line : line + vecs, c : c + LANES])
            turned = jnp.concatenate(parts, axis=0).T
            field[m, c : c + LANES, :] = turned
            if c == 0:
                edges[0, m * RIM_C : (m + 1) * RIM_C, :] = turned[:RIM_C]
            if c == cols - LANES:
                edges[1, m * RIM_C : (m + 1) * RIM_C, :] = turned[LANES - RIM_C :]
    at = depth * RIM_C
    edges[0, at : at + padded, :] = dis_pad[:, :LANES]
    edges[1, at : at + padded, :] = dis_pad[:, cols - LANES :]


def energy_kernel(vecs, dis_pad, out):
    padded, cols = dis_pad.shape
    groups = LANES // vecs
    depth = padded // groups
    for m in range(depth):
        for c in range(0, cols, LANES):
            parts = [
                jnp.broadcast_to(dis_pad[g * depth + m : g * depth + m + 1, c : c + LANES], (vecs, LANES))
                for g in range(groups)
            ]
            out[m, c : c + LANES, :] = (jnp.concatenate(parts, axis=0) * (2.0 / SCALE)).T


def step_kernel(rows, vecs, field, energy, left, right, last, stats, buf, ene, acc_ref):
    depth, cols, _ = field.shape
    padded = rows + 2 * RIM_R
    groups = LANES // vecs
    lead = 8 + RIM_C
    at = depth * RIM_C
    for m in range(depth):
        buf[0, m, 8:lead, :] = left[m * RIM_C : (m + 1) * RIM_C, :]
        buf[0, m, lead : lead + cols, :] = field[m]
        buf[0, m, lead + cols : lead + cols + RIM_C, :] = right[m * RIM_C : (m + 1) * RIM_C, :]
        for side, ref, first in ((0, left, LANES - RIM_C), (1, right, 0)):
            parts = [
                jnp.broadcast_to(ref[at + g * depth + m : at + g * depth + m + 1, :], (vecs, LANES))
                for g in range(groups)
            ]
            turned = (jnp.concatenate(parts, axis=0) * (2.0 / SCALE)).T
            ene[side, m] = turned[first : first + RIM_C]
    odd = lax.broadcasted_iota(jnp.int32, (8, LANES), 0) % 2 == 1
    group = lax.broadcasted_iota(jnp.int32, (8, LANES), 1) // vecs
    tiles = (cols + 2 * RIM_C) // 8
    zero = jnp.zeros((8, LANES), jnp.float32)

    def own(parts):
        total = zero
        for m in range(depth):
            place = group * depth + m
            kept = (place >= RIM_R) & (place < RIM_R + rows)
            total = total + jnp.where(kept, parts[m], 0.0)
        return total

    def advance(now, then, first):
        squares, crosses, start = [zero] * depth, [zero] * depth, [zero] * depth
        for t in range(tiles):
            c = 8 + 8 * t
            mine = 0 < t < tiles - 1
            here = [buf[now, m, c : c + 8, :] for m in range(depth)]
            over = pltpu.roll(here[depth - 1], vecs, 1)
            under = pltpu.roll(here[0], LANES - vecs, 1)
            for m in range(depth):
                above = here[m - 1] if m > 0 else over
                below = here[m + 1] if m < depth - 1 else under
                vertical = jnp.where(odd, below, above) if m % 2 else jnp.where(odd, above, below)
                near = buf[now, m, c - 1 : c + 7, :] + buf[now, m, c + 1 : c + 9, :] + vertical
                if mine:
                    e = energy[m, c - lead : c - lead + 8, :]
                else:
                    e = ene[0 if t == 0 else 1, m]
                latest = e * here[m] - (2.0 / SCALE) * near
                if first:
                    latest = 0.5 * latest
                else:
                    latest = latest - buf[then, m, c : c + 8, :]
                buf[then, m, c : c + 8, :] = latest
                if mine:
                    squares[m] = squares[m] + latest * latest
                    crosses[m] = crosses[m] + latest * here[m]
                    if first:
                        start[m] = start[m] + here[m] * here[m]
        return squares, crosses, start

    squares, crosses, start = advance(0, 1, True)
    acc_ref[0] = own(start)
    acc_ref[1] = own(crosses)
    acc_ref[2] = own(squares)

    def body(n, _):
        now = lax.rem(n, 2)
        squares, crosses, _ = advance(now, 1 - now, False)
        acc_ref[2 * n + 1] = own(crosses)
        acc_ref[2 * n + 2] = own(squares)
        return 0

    lax.fori_loop(1, STEPS, body, 0)
    lane = lax.broadcasted_iota(jnp.int32, (8, LANES), 1)
    total = zero
    for k in range(2 * STEPS + 1):
        total = total + jnp.where(lane == k, jnp.sum(acc_ref[k], axis=1, keepdims=True), 0.0)
    stats[...] = jnp.broadcast_to(jnp.sum(total, axis=0, keepdims=True), (8, LANES))
    for m in range(depth):
        last[0, m] = buf[(STEPS - 1) % 2, m, lead : lead + cols, :]
        last[1, m] = buf[STEPS % 2, m, lead : lead + cols, :]


def unturn_kernel(rows, vecs, last, prev_out, last_out, flat, sem):
    depth, cols = last.shape[1:3]
    groups = LANES // vecs
    copies = []
    for k, out in ((0, prev_out), (1, last_out)):
        for m in range(depth):
            for c in range(0, cols, LANES):
                turned = last[k, m, c : c + LANES, :].T
                for g in range(groups):
                    r = g * depth + m - RIM_R
                    if 0 <= r < rows:
                        flat[k, r, :, c : c + LANES] = turned[g * vecs : (g + 1) * vecs]
            for g in range(groups):
                r = g * depth + m - RIM_R
                if 0 <= r < rows:
                    copy = pltpu.make_async_copy(flat.at[k, r], out.at[:, r, :], sem.at[k, r])
                    copy.start()
                    copies.append(copy)
    for copy in copies:
        copy.wait()


def shift(array, axis, by):
    count = lax.axis_size(axis)
    return lax.ppermute(array, axis, [(i, (i + by) % count) for i in range(count)])


def body(vectors, disorder):
    vecs, rows, cols = vectors.shape
    f32 = jnp.float32
    groups = LANES // vecs
    padded = rows + 2 * RIM_R
    depth = padded // groups
    assert vecs * groups == LANES and depth * groups == padded and depth % 2 == 0
    assert rows % 8 == 0 and rows > 2 * RIM_R and cols % LANES == 0
    rim = jax.ShapeDtypeStruct((RIM_R * vecs + 8, cols), f32)
    mid = jax.ShapeDtypeStruct(((rows - 2 * RIM_R) * vecs, cols), f32)
    top, mid, bot = pl.pallas_call(
        pack_kernel,
        out_shape=(rim, mid, rim),
        in_specs=[ANY, VMEM],
        out_specs=(VMEM, VMEM, VMEM),
        scratch_shapes=[pltpu.SemaphoreType.DMA((rows,))],
        name="pack",
    )(vectors, disorder)
    lo = shift(bot, "row", 1)
    hi = shift(top, "row", -1)
    field, edges, dis_pad = pl.pallas_call(
        functools.partial(turn_kernel, rows, vecs),
        out_shape=(
            jax.ShapeDtypeStruct((depth, cols, LANES), f32),
            jax.ShapeDtypeStruct((2, depth * RIM_C + padded, LANES), f32),
            jax.ShapeDtypeStruct((padded, cols), f32),
        ),
        in_specs=[VMEM] * 6,
        out_specs=(VMEM,) * 3,
        name="turn",
    )(lo, top, mid, bot, hi, disorder)
    if lax.axis_size("col") == 2:
        other = shift(edges, "col", 1)
        left, right = other[1], other[0]
    else:
        left, right = shift(edges[1], "col", 1), shift(edges[0], "col", -1)
    energy = pl.pallas_call(
        functools.partial(energy_kernel, vecs),
        out_shape=jax.ShapeDtypeStruct((depth, cols, LANES), f32),
        in_specs=[VMEM],
        out_specs=VMEM,
        name="energy",
    )(dis_pad)
    wide = cols + 2 * RIM_C + 16
    last, stats = pl.pallas_call(
        functools.partial(step_kernel, rows, vecs),
        out_shape=(
            jax.ShapeDtypeStruct((2, depth, cols, LANES), f32),
            jax.ShapeDtypeStruct((8, LANES), f32),
        ),
        in_specs=[VMEM] * 4,
        out_specs=(VMEM, VMEM),
        scratch_shapes=[
            pltpu.VMEM((2, depth, wide, LANES), f32),
            pltpu.VMEM((2, depth, RIM_C, LANES), f32),
            pltpu.VMEM((2 * STEPS + 1, 8, LANES), f32),
        ],
        name="steps",
    )(field, energy, left, right)
    older, newer = pl.pallas_call(
        functools.partial(unturn_kernel, rows, vecs),
        out_shape=(jax.ShapeDtypeStruct(vectors.shape, f32),) * 2,
        in_specs=[VMEM],
        out_specs=(ANY, ANY),
        scratch_shapes=[
            pltpu.VMEM((2, rows, vecs, cols), f32),
            pltpu.SemaphoreType.DMA((2, rows)),
        ],
        name="unturn",
    )(last)
    for axis in ("row", "col", "grp"):
        count, reach = lax.axis_size(axis), 1
        assert count & (count - 1) == 0
        while reach < count:
            stats = stats + lax.ppermute(stats, axis, [(i, i ^ reach) for i in range(count)])
            reach *= 2
    sites = vecs * rows * cols
    for axis in AXES:
        sites *= lax.axis_size(axis)
    sums = stats[0, : 2 * STEPS + 1] / float(sites)
    index = jnp.arange(2 * STEPS + 1)
    base = jnp.where(index % 2 == 0, sums[0], sums[1])
    moments = jnp.where(index < 2, sums, 2.0 * sums - base)
    return older, newer, moments


def solution(mesh):
    return jax.shard_map(
        body,
        mesh=mesh,
        in_specs=(P("grp", "row", "col"), P("row", "col")),
        out_specs=(P("grp", "row", "col"), P("grp", "row", "col"), P()),
        check_vma=False,
    )
```

time: 163 us -> 50.7 us (0.31)
  blocking collectives: 40.1 us -> 0 us
  waiting for transfers between devices: 44.3 us -> 12.2 us
  Pallas kernels: 0 us -> 19.2 us
  between operations: 19.6 us -> 0.68 us
  other arithmetic: 17.3 us -> 2.47 us
  local copies, waits for them, and re-layouts: 16.7 us -> 1.95 us
  starting transfers between devices: 24.2 us -> 13.7 us
    psum x1 -> x0, blocking collectives: 40.1 us -> none  [body(): total_squares = [lax.psum(squares[0], ('grp', 'row', 'col'))]]
    ppermute x16 -> x8, waiting for transfers between devices: 44.3 us -> 12.2 us  [the longest x5 8.28 us: body(): lax.ppermute(stats, axis, [(i, i ^ reach) for i in range(count)])]
    pallas_call x0 -> x5, Pallas kernels: none -> 19.2 us  [the longest x1 8.68 us: body(): pl.pallas_call(functools.partial(step_kernel, rows, vecs), out_shape=(jax...]
    another operation x3 -> x0, local copies, waits for them, and re-layouts: 12.8 us -> none  [the longest x1 5.71 us: body(): total_squares = jnp.stack(total_squares)]
    ppermute x16 -> x8, starting transfers between devices: 24.2 us -> 13.7 us  [the longest x5 7.08 us: body(): lax.ppermute(stats, axis, [(i, i ^ reach) for i in range(count)])]
    sub x5 -> x0, other arithmetic: 8.54 us -> none  [body(): latest = 2.0 * advance(padded_new) - padded_old[:, 1:-1, 1:-1]]
    concatenate x7 -> x0, other arithmetic: 3.66 us -> none  [extended(): block = jnp.concatenate([low, block, high], axis=dim)]
    slice x16 -> x1, local copies, waits for them, and re-layouts: 3.89 us -> 0.6 us  [body(): base = jnp.where(index % 2 == 0, sums[0], sums[1])]
  transfers between devices with their start and end apart: 16 -> 8, of which waited for: 8 -> 6; matrix products, arithmetic and copies ran while one was open for 3% -> 0% of each run, Pallas kernels for 0% -> 11%
where the time goes in v1:
time: 50.7 us; the launch traced here: 50.3 us
  Pallas kernels  19.2 us (38%)
  starting transfers between devices  13.7 us (27%)
  waiting for transfers between devices  12.2 us (24%)
  other arithmetic  2.47 us (5%)
  local copies, waits for them, and re-layouts  1.95 us (4%)
  between operations  0.68 us (1%)
    pallas_call x1, Pallas kernels, body(): pl.pallas_call(functools.partial(step_kernel, rows, vecs), out_shape=(jax...  8.68 us
    ppermute x5, waiting for transfers between devices, body(): lax.ppermute(stats, axis, [(i, i ^ reach) for i in range(count)])  8.28 us
    ppermute x5, starting transfers between devices, body(): lax.ppermute(stats, axis, [(i, i ^ reach) for i in range(count)])  7.08 us
    ppermute x3, starting transfers between devices, shift(): lax.ppermute(array, axis, [(i, (i + by) % count) for i in range(count)])  6.65 us
    ppermute x3, waiting for transfers between devices, shift(): lax.ppermute(array, axis, [(i, (i + by) % count) for i in range(count)])  3.97 us
    pallas_call x1, Pallas kernels, body(): pl.pallas_call(functools.partial(unturn_kernel, rows, vecs), out_shape=(j...  3.51 us
    pallas_call x1, Pallas kernels, body(): pl.pallas_call(pack_kernel, out_shape=(rim, mid, rim), in_specs=[ANY, VME...  2.71 us
    pallas_call x1, Pallas kernels, body(): pl.pallas_call(functools.partial(turn_kernel, rows, vecs), out_shape=(jax...  2.39 us
  transfers between devices with their start and end apart: 8, of which 6 were waited for; matrix products, arithmetic and copies ran while one was open for 0% of the time, Pallas kernels for 11%

profile of v1, /device:TPU:0, one launch (start us, length us, event | category | flops | bytes accessed | tf_op | source)
XLA Modules:
  0.0 50.3 jit_solution(17697553578984429523)
XLA Ops:
  0.6 2.7 %pack.1 = (f32[136,256]{1,0:T(8,128)}, f32[256,256]{1,0:T(8,128)}, f32[136,256]{1,0:T(8,128)}) custom-call(f32[32,16,256]{2,1,0:T(8,128)} %vec.1, f32[16,256]{1,0:T(8,128)} %dis.3), custom_call_target="tpu_custom_call" | custom-call | tf_op jit(solution)/shard_map/pack/pallas_call | solution.py:206
  3.3 0.5 %collective-permute-start = (f32[136,256]{1,0:T(8,128)}, f32[136,256]{1,0:T(8,128)S(1)}, u32[]{:S(2)}, u32[]{:S(2)}) collective-permute-start(f32[136,256]{1,0:T(8,128)} %get-tuple-element.13.bot), channel_id=1, source_target_pairs={{0,2},{2,4},{4,6},{6,8},{8,10},{10,12},{12,14},{14,0},{1,3},{3,5},... | collective-permute-start | bytes 417800 | tf_op jit(solution)/shard_map/ppermute | solution.py:193
  3.9 4.1 %collective-permute-start.1 = (f32[136,256]{1,0:T(8,128)}, f32[136,256]{1,0:T(8,128)S(1)}, u32[]{:S(2)}, u32[]{:S(2)}) collective-permute-start(f32[136,256]{1,0:T(8,128)} %get-tuple-element.14.top), channel_id=1, source_target_pairs={{0,14},{2,0},{4,2},{6,4},{8,6},{10,8},{12,10},{14,12},{1,15},{3,1}... | collective-permute-start | bytes 417800 | tf_op jit(solution)/shard_map/ppermute | solution.py:193
  8.0 3.0 %collective-permute-done.lo = f32[136,256]{1,0:T(8,128)S(1)} collective-permute-done((f32[136,256]{1,0:T(8,128)}, f32[136,256]{1,0:T(8,128)S(1)}, u32[]{:S(2)}, u32[]{:S(2)}) %collective-permute-start) | collective-permute-done | bytes 139296 | tf_op jit(solution)/shard_map/ppermute | solution.py:193
  11.0 0.0 copy-start
  11.0 0.0 collective-permute-done.1.hi
  11.0 0.0 copy-start.1
  11.0 0.6 %copy-done = f32[136,256]{1,0:T(8,128)} copy-done((f32[136,256]{1,0:T(8,128)}, f32[136,256]{1,0:T(8,128)S(1)}, u32[]{:S(2)}) %copy-start) | copy-done | bytes 139288
  11.6 0.1 copy-done.1
  11.7 2.4 %turn.1 = (f32[6,256,128]{2,1,0:T(8,128)}, f32[2,72,128]{2,1,0:T(8,128)}, f32[24,256]{1,0:T(8,128)}) custom-call(f32[136,256]{1,0:T(8,128)} %copy-done, f32[136,256]{1,0:T(8,128)} %get-tuple-element.14.top, f32[256,256]{1,0:T(8,128)} %get-tuple-element.15.mid, f32[136,256]{1,0:T(8,128)} %get-tuple-element.13.bot, f32[136,256]{1,0:T(8,128)} %copy-done.1, ...), custom_call_target="tpu_custom_call" | custom-call | tf_op jit(solution)/shard_map/turn/pallas_call | solution.py:216
  14.1 2.0 %collective-permute-start.2 = (f32[2,72,128]{2,1,0:T(8,128)}, f32[2,72,128]{2,1,0:T(8,128)S(1)}, u32[]{:S(2)}, u32[]{:S(2)}) collective-permute-start(f32[2,72,128]{2,1,0:T(8,128)} %get-tuple-element.18), channel_id=1, source_target_pairs={{0,1},{1,0},{2,3},{3,2},{4,5},{5,4},{6,7},{7,6},{8,9},{9,8},{10,11... | collective-permute-start | bytes 221192 | tf_op jit(solution)/shard_map/ppermute | solution.py:193
  16.1 1.9 %energy.1 = f32[6,256,128]{2,1,0:T(8,128)} custom-call(f32[24,256]{1,0:T(8,128)} %get-tuple-element.17.dis_pad), custom_call_target="tpu_custom_call" | custom-call | tf_op jit(solution)/shard_map/energy/pallas_call | solution.py:232
  18.0 1.0 %collective-permute-done.2 = f32[2,72,128]{2,1,0:T(8,128)S(1)} collective-permute-done((f32[2,72,128]{2,1,0:T(8,128)}, f32[2,72,128]{2,1,0:T(8,128)S(1)}, u32[]{:S(2)}, u32[]{:S(2)}) %collective-permute-start.2) | collective-permute-done | bytes 73760 | tf_op jit(solution)/shard_map/ppermute | solution.py:193
  19.0 0.6 %slice_bitcast_fusion = (f32[72,128]{1,0:T(8,128)}, f32[72,128]{1,0:T(8,128)}) fusion(f32[2,72,128]{2,1,0:T(8,128)S(1)} %collective-permute-done.2), kind=kLoop, calls=%fused_computation | loop fusion | bytes 147456 | tf_op jit(solution)/shard_map/squeeze | solution.py:229
  19.6 8.7 %steps.1 = (f32[2,6,256,128]{3,2,1,0:T(8,128)}, f32[8,128]{1,0:T(8,128)}) custom-call(f32[6,256,128]{2,1,0:T(8,128)} %get-tuple-element.16.field, f32[6,256,128]{2,1,0:T(8,128)} %energy.1, f32[72,128]{1,0:T(8,128)} %get-tuple-element.24.left, f32[72,128]{1,0:T(8,128)} %get-tuple-element.23.right), custom_call_target="tpu_custom_call" | custom-call | tf_op jit(solution)/shard_map/steps/pallas_call | solution.py:240
  28.3 0.3 collective-permute-start.3
  28.6 1.1 %collective-permute-done.3 = f32[8,128]{1,0:T(8,128)S(1)} collective-permute-done((f32[8,128]{1,0:T(8,128)}, f32[8,128]{1,0:T(8,128)S(1)}, u32[]{:S(2)}, u32[]{:S(2)}) %collective-permute-start.3) | collective-permute-done | bytes 4128 | tf_op jit(solution)/shard_map/ppermute | solution.py:270
  29.7 0.7 %add.21 = f32[8,128]{1,0:T(8,128)S(1)} add(f32[8,128]{1,0:T(8,128)} %get-tuple-element.22, f32[8,128]{1,0:T(8,128)S(1)} %collective-permute-done.3) | non-fusion elementwise | flops 1024 | bytes 12288 | tf_op jit(solution)/shard_map/add | solution.py:270
  30.3 1.4 %collective-permute-start.4 = (f32[8,128]{1,0:T(8,128)S(1)}, f32[8,128]{1,0:T(8,128)S(1)}, u32[]{:S(2)}, u32[]{:S(2)}) collective-permute-start(f32[8,128]{1,0:T(8,128)S(1)} %add.21), channel_id=1, source_target_pairs={{0,4},{2,6},{4,0},{6,2},{8,12},{10,14},{12,8},{14,10},{1,5},{3,7},... | collective-permute-start | bytes 12296 | tf_op jit(solution)/shard_map/ppermute | solution.py:270
  31.7 2.2 %collective-permute-done.4 = f32[8,128]{1,0:T(8,128)S(1)} collective-permute-done((f32[8,128]{1,0:T(8,128)S(1)}, f32[8,128]{1,0:T(8,128)S(1)}, u32[]{:S(2)}, u32[]{:S(2)}) %collective-permute-start.4) | collective-permute-done | bytes 4128 | tf_op jit(solution)/shard_map/ppermute | solution.py:270
  34.0 1.1 %collective-permute-start.5 = (f32[8,128]{1,0:T(8,128)S(1)}, f32[8,128]{1,0:T(8,128)S(1)}, u32[]{:S(2)}, u32[]{:S(2)}) collective-permute-start(f32[8,128]{1,0:T(8,128)S(1)} %add.22), channel_id=1, source_target_pairs={{0,8},{2,10},{4,12},{6,14},{8,0},{10,2},{12,4},{14,6},{1,9},{3,11}... | collective-permute-start | bytes 12296 | tf_op jit(solution)/shard_map/ppermute | solution.py:270
  35.1 3.4 %collective-permute-done.5 = f32[8,128]{1,0:T(8,128)S(1)} collective-permute-done((f32[8,128]{1,0:T(8,128)S(1)}, f32[8,128]{1,0:T(8,128)S(1)}, u32[]{:S(2)}, u32[]{:S(2)}) %collective-permute-start.5) | collective-permute-done | bytes 4128 | tf_op jit(solution)/shard_map/ppermute | solution.py:270
  38.5 2.3 %collective-permute-start.6 = (f32[8,128]{1,0:T(8,128)S(1)}, f32[8,128]{1,0:T(8,128)S(1)}, u32[]{:S(2)}, u32[]{:S(2)}) collective-permute-start(f32[8,128]{1,0:T(8,128)S(1)} %add.23), channel_id=1, source_target_pairs={{0,1},{1,0},{2,3},{3,2},{4,5},{5,4},{6,7},{7,6},{8,9},{9,8},{10,11... | collective-permute-start | bytes 12296 | tf_op jit(solution)/shard_map/ppermute | solution.py:270
  40.8 1.6 %collective-permute-done.6 = f32[8,128]{1,0:T(8,128)S(1)} collective-permute-done((f32[8,128]{1,0:T(8,128)S(1)}, f32[8,128]{1,0:T(8,128)S(1)}, u32[]{:S(2)}, u32[]{:S(2)}) %collective-permute-start.6) | collective-permute-done | bytes 4128 | tf_op jit(solution)/shard_map/ppermute | solution.py:270
  42.3 2.0 %collective-permute-start.7 = (f32[8,128]{1,0:T(8,128)S(1)}, f32[8,128]{1,0:T(8,128)S(1)}, u32[]{:S(2)}, u32[]{:S(2)}) collective-permute-start(f32[8,128]{1,0:T(8,128)S(1)} %add.24), channel_id=1, source_target_pairs={{0,16},{16,0},{1,17},{17,1},{2,18},{18,2},{3,19},{19,3},{4,20},{20... | collective-permute-start | bytes 12296 | tf_op jit(solution)/shard_map/ppermute | solution.py:270
  44.3 3.5 %unturn.1 = (f32[32,16,256]{2,1,0:T(8,128)}, f32[32,16,256]{2,1,0:T(8,128)}) custom-call(f32[2,6,256,128]{3,2,1,0:T(8,128)} %get-tuple-element.19.last), custom_call_target="tpu_custom_call" | custom-call | tf_op jit(solution)/shard_map/unturn/pallas_call | solution.py:255
  47.9 0.0 collective-permute-done.7
  47.9 0.6 %fusion.1 = (f32[1,1]{1,0:T(1,128)}, f32[1,1]{1,0:T(1,128)}) fusion(f32[1,17]{1,0:T(1,128)S(1)} %slice_multiply_fusion), kind=kLoop, calls=%fused_computation.7 | loop fusion | bytes 16 | tf_op jit(solution)/shard_map/slice | solution.py:277
  48.5 1.8 %compare_select_fusion.1 = f32[17]{0:T(128)} fusion(f32[8,128]{1,0:T(8,128)S(1)} %add.25, f32[]{:T(128)} %bitcast.5, f32[]{:T(128)} %bitcast.4), kind=kLoop, calls=%fused_computation.4 | loop fusion | flops 221 | bytes 144 | tf_op jit(solution)/shard_map/jit(_where)/select_n | solution.py:278
  (5 shorter events, 0.0 us)
Async XLA Ops:
  3.3 7.6 %collective-permute-start = (f32[136,256]{1,0:T(8,128)}, f32[136,256]{1,0:T(8,128)S(1)}, u32[]{:S(2)}, u32[]{:S(2)}) collective-permute-start(f32[136,256]{1,0:T(8,128)} %get-tuple-element.13.bot), channel_id=1, source_target_pairs={{0,2},{2,4},{4,6},{6,8},{8,10},{10,12},{12,14},{14,0},{1,3},{3,5},... | collective-permute-start | bytes 417800 | tf_op jit(solution)/shard_map/ppermute | solution.py:193
  3.9 7.1 %collective-permute-start.1 = (f32[136,256]{1,0:T(8,128)}, f32[136,256]{1,0:T(8,128)S(1)}, u32[]{:S(2)}, u32[]{:S(2)}) collective-permute-start(f32[136,256]{1,0:T(8,128)} %get-tuple-element.14.top), channel_id=1, source_target_pairs={{0,14},{2,0},{4,2},{6,4},{8,6},{10,8},{12,10},{14,12},{1,15},{3,1}... | collective-permute-start | bytes 417800 | tf_op jit(solution)/shard_map/ppermute | solution.py:193
  11.0 0.6 %copy-start = (f32[136,256]{1,0:T(8,128)}, f32[136,256]{1,0:T(8,128)S(1)}, u32[]{:S(2)}) copy-start(f32[136,256]{1,0:T(8,128)S(1)} %collective-permute-done.lo) | copy-start | bytes 417796
  11.0 0.7 %copy-start.1 = (f32[136,256]{1,0:T(8,128)}, f32[136,256]{1,0:T(8,128)S(1)}, u32[]{:S(2)}) copy-start(f32[136,256]{1,0:T(8,128)S(1)} %collective-permute-done.1.hi) | copy-start | bytes 417796
  14.1 4.9 %collective-permute-start.2 = (f32[2,72,128]{2,1,0:T(8,128)}, f32[2,72,128]{2,1,0:T(8,128)S(1)}, u32[]{:S(2)}, u32[]{:S(2)}) collective-permute-start(f32[2,72,128]{2,1,0:T(8,128)} %get-tuple-element.18), channel_id=1, source_target_pairs={{0,1},{1,0},{2,3},{3,2},{4,5},{5,4},{6,7},{7,6},{8,9},{9,8},{10,11... | collective-permute-start | bytes 221192 | tf_op jit(solution)/shard_map/ppermute | solution.py:193
  28.3 1.4 %collective-permute-start.3 = (f32[8,128]{1,0:T(8,128)}, f32[8,128]{1,0:T(8,128)S(1)}, u32[]{:S(2)}, u32[]{:S(2)}) collective-permute-start(f32[8,128]{1,0:T(8,128)} %get-tuple-element.22), channel_id=1, source_target_pairs={{0,2},{2,0},{4,6},{6,4},{8,10},{10,8},{12,14},{14,12},{1,3},{3,1},... | collective-permute-start | bytes 12296 | tf_op jit(solution)/shard_map/ppermute | solution.py:270
  30.3 3.6 %collective-permute-start.4 = (f32[8,128]{1,0:T(8,128)S(1)}, f32[8,128]{1,0:T(8,128)S(1)}, u32[]{:S(2)}, u32[]{:S(2)}) collective-permute-start(f32[8,128]{1,0:T(8,128)S(1)} %add.21), channel_id=1, source_target_pairs={{0,4},{2,6},{4,0},{6,2},{8,12},{10,14},{12,8},{14,10},{1,5},{3,7},... | collective-permute-start | bytes 12296 | tf_op jit(solution)/shard_map/ppermute | solution.py:270
  34.0 4.5 %collective-permute-start.5 = (f32[8,128]{1,0:T(8,128)S(1)}, f32[8,128]{1,0:T(8,128)S(1)}, u32[]{:S(2)}, u32[]{:S(2)}) collective-permute-start(f32[8,128]{1,0:T(8,128)S(1)} %add.22), channel_id=1, source_target_pairs={{0,8},{2,10},{4,12},{6,14},{8,0},{10,2},{12,4},{14,6},{1,9},{3,11}... | collective-permute-start | bytes 12296 | tf_op jit(solution)/shard_map/ppermute | solution.py:270
  38.5 3.9 %collective-permute-start.6 = (f32[8,128]{1,0:T(8,128)S(1)}, f32[8,128]{1,0:T(8,128)S(1)}, u32[]{:S(2)}, u32[]{:S(2)}) collective-permute-start(f32[8,128]{1,0:T(8,128)S(1)} %add.23), channel_id=1, source_target_pairs={{0,1},{1,0},{2,3},{3,2},{4,5},{5,4},{6,7},{7,6},{8,9},{9,8},{10,11... | collective-permute-start | bytes 12296 | tf_op jit(solution)/shard_map/ppermute | solution.py:270
  42.3 5.5 %collective-permute-start.7 = (f32[8,128]{1,0:T(8,128)S(1)}, f32[8,128]{1,0:T(8,128)S(1)}, u32[]{:S(2)}, u32[]{:S(2)}) collective-permute-start(f32[8,128]{1,0:T(8,128)S(1)} %add.24), channel_id=1, source_target_pairs={{0,16},{16,0},{1,17},{17,1},{2,18},{18,2},{3,19},{19,3},{4,20},{20... | collective-permute-start | bytes 12296 | tf_op jit(solution)/shard_map/ppermute | solution.py:270

commit v2 on v0

v2 whole, which is shorter than its diff:
```python
import functools

import jax
import jax.numpy as jnp
from jax import lax
from jax.experimental import pallas as pl
from jax.experimental.pallas import tpu as pltpu
from jax.sharding import PartitionSpec as P

STEPS = 8
SCALE = 4.6
RIM_R = (STEPS + 1) // 2
RIM_C = STEPS
LANES = 128
AXES = ("grp", "row", "col")
SUMS = 2 * STEPS + 1

VMEM = pl.BlockSpec(memory_space=pltpu.VMEM)
HBM = pl.BlockSpec(memory_space=pltpu.HBM)
F32 = jnp.float32


def pack_kernel(vec, dis, top, bot, vec_out, dis_out, sem):
    vecs, rows, _ = vec.shape
    parts = 4
    some = vecs // parts
    copies = [pltpu.make_async_copy(dis, dis_out, sem.at[parts])]
    for k in range(parts):
        here = pl.ds(k * some, some)
        copies.append(pltpu.make_async_copy(vec.at[here], vec_out.at[here], sem.at[k]))
    for copy in copies:
        copy.start()
    copies[0].wait()
    top[RIM_R * vecs :, :] = dis_out[:8, :]
    bot[RIM_R * vecs :, :] = dis_out[rows - 8 :, :]
    for k in range(parts):
        copies[1 + k].wait()
        for r in range(RIM_R):
            line = r * vecs + k * some
            top[line : line + some, :] = vec_out[k * some : (k + 1) * some, r, :]
            bot[line : line + some, :] = vec_out[k * some : (k + 1) * some, rows - RIM_R + r, :]


def turn_kernel(lo, hi, vec, dis, field, edges, dis_turned):
    vecs, rows, cols = vec.shape
    groups = LANES // vecs
    padded = rows + 2 * RIM_R
    depth = padded // groups
    at = RIM_R * vecs

    def lines(p, c):
        if p < RIM_R:
            return lo[p * vecs : (p + 1) * vecs, c : c + LANES]
        if p < RIM_R + rows:
            return vec[:, p - RIM_R, c : c + LANES]
        p -= RIM_R + rows
        return hi[p * vecs : (p + 1) * vecs, c : c + LANES]

    ends = ((0, 0), (cols - LANES, LANES - RIM_C))
    for c in range(0, cols, LANES):
        for m in range(depth):
            turned = jnp.concatenate([lines(g * depth + m, c) for g in range(groups)], axis=0).T
            field[m, 8 + c : 8 + c + LANES, :] = turned
            for side, (place, first) in enumerate(ends):
                if c == place:
                    edges[side, m * RIM_C : (m + 1) * RIM_C, :] = turned[first : first + RIM_C]
        block = [
            lo[at + 8 - RIM_R : at + 8, c : c + LANES],
            dis[:, c : c + LANES],
            hi[at : at + RIM_R, c : c + LANES],
            jnp.zeros((LANES - padded, LANES), F32),
        ]
        turned = jnp.concatenate(block, axis=0).T * (2.0 / SCALE)
        dis_turned[c : c + LANES, :] = turned
        for side, (place, first) in enumerate(ends):
            if c == place:
                edges[side, depth * RIM_C :, :] = turned[first : first + RIM_C]


def spread_rows(tile, m, vecs, depth):
    index = lax.broadcasted_iota(jnp.int32, (8, LANES), 1) // vecs * depth + m
    return jnp.take_along_axis(tile, index, axis=1)


def advance(depth, vecs, now, then, out, energy, tiles, counted, sums):
    odd = lax.broadcasted_iota(jnp.int32, (8, LANES), 0) % 2 == 1
    for t in tiles:
        here = [now(m, t, 0) for m in range(depth)]
        over = pltpu.roll(here[depth - 1], vecs, 1)
        under = pltpu.roll(here[0], LANES - vecs, 1)
        for m in range(depth):
            above = here[m - 1] if m > 0 else over
            below = here[m + 1] if m < depth - 1 else under
            vertical = jnp.where(odd, below, above) if m % 2 else jnp.where(odd, above, below)
            near = (now(m, t, -1) + now(m, t, 1)) + vertical
            latest = energy(m, t) * here[m] - (2.0 / SCALE) * near
            latest = 0.5 * latest if then is None else latest - then(m, t, 0)
            out(m, t, latest)
            if t in counted:
                sums["s"][m] = sums["s"][m] + latest * latest
                sums["r"][m] = sums["r"][m] + latest * here[m]
                if then is None:
                    sums["0"][m] = sums["0"][m] + here[m] * here[m]


def fresh(depth):
    zero = jnp.zeros((8, LANES), F32)
    return {name: [zero] * depth for name in "sr0"}


def own(parts, rows, vecs):
    depth = len(parts)
    group = lax.broadcasted_iota(jnp.int32, (8, LANES), 1) // vecs
    total = jnp.zeros((8, LANES), F32)
    for m in range(depth):
        place = group * depth + m
        kept = (place >= RIM_R) & (place < RIM_R + rows)
        total = total + jnp.where(kept, parts[m], 0.0)
    return total


def chain(field, odd, even):
    result = [(field, None, odd), (odd, field, even)]
    for n in range(2, STEPS):
        now, other = (odd, even) if n % 2 else (even, odd)
        result.append((now, other, other))
    return result


def inner_kernel(rows, vecs, cols, field, dis_turned, odd, even, partial, ene):
    depth = field.shape[0]
    tiles = cols // 8
    for t in range(tiles):
        tile = dis_turned[8 * t : 8 * t + 8, :]
        for m in range(depth):
            ene[m, 8 * t : 8 * t + 8, :] = spread_rows(tile, m, vecs, depth)

    def reader(ref):
        return lambda m, t, by: ref[m, 8 + 8 * t + by : 16 + 8 * t + by, :]

    def writer(ref):
        def write(m, t, value):
            ref[m, 8 + 8 * t : 16 + 8 * t, :] = value

        return write

    for n, (now, then, out) in enumerate(chain(field, odd, even)):
        sums = fresh(depth)
        advance(
            depth,
            vecs,
            reader(now),
            None if then is None else reader(then),
            writer(out),
            lambda m, t: ene[m, 8 * t : 8 * t + 8, :],
            range(tiles),
            range(1, tiles - 1),
            sums,
        )
        if n == 0:
            partial[0] = own(sums["0"], rows, vecs)
        partial[2 * n + 1] = own(sums["r"], rows, vecs)
        partial[2 * n + 2] = own(sums["s"], rows, vecs)


def edge_kernel(
    rows, vecs, cols, places, sites, field, dis_turned, left, right, partial, ends, spread, start, odd, even, ene
):
    depth = field.shape[0]
    at = depth * RIM_C
    for side, rim, rim_at, mine in ((0, left, 0, (0, 1)), (1, right, 2, (cols // 8 - 2, cols // 8 - 1))):
        order = [None, *mine] if rim_at == 0 else [*mine, None]
        for k, t in enumerate(order):
            if t is None:
                tile = rim[places[side], at : at + 8, :]
            else:
                tile = dis_turned[8 * t : 8 * t + 8, :]
            for m in range(depth):
                if t is None:
                    value = rim[places[side], m * RIM_C : (m + 1) * RIM_C, :]
                else:
                    value = field[m, 8 + 8 * t : 16 + 8 * t, :]
                start[side, m, 8 + 8 * k : 16 + 8 * k, :] = value
                ene[side, m, 8 * k : 8 * k + 8, :] = spread_rows(tile, m, vecs, depth)

    def reader(ref):
        return lambda m, t, by: ref[t[0], m, 8 + 8 * t[1] + by : 16 + 8 * t[1] + by, :]

    def writer(ref):
        def write(m, t, value):
            ref[t[0], m, 8 + 8 * t[1] : 16 + 8 * t[1], :] = value

        return write

    middle = ((0, 1), (1, 1))
    every = [(side, k) for side in (0, 1) for k in (0, 1, 2)]
    lane = lax.broadcasted_iota(jnp.int32, (8, LANES), 1)
    total = jnp.zeros((8, LANES), F32)
    first = []

    def place(total, k, parts):
        value = jnp.sum(partial[k] + own(parts, rows, vecs), axis=1, keepdims=True)
        if k < 2:
            first.append(jnp.sum(value, axis=0, keepdims=True))
        return total + jnp.where(lane == k, value, 0.0)

    for n, (now, then, out) in enumerate(chain(start, odd, even)):
        sums = fresh(depth)
        advance(
            depth,
            vecs,
            reader(now),
            None if then is None else reader(then),
            writer(out),
            lambda m, t: ene[t[0], m, 8 * t[1] : 8 * t[1] + 8, :],
            every if n < STEPS - 1 else middle,
            middle,
            sums,
        )
        if n == 0:
            total = place(total, 0, sums["0"])
        total = place(total, 2 * n + 1, sums["r"]) if n < STEPS else total
        total = place(total, 2 * n + 2, sums["s"])
    line = lane[:1]
    values = jnp.sum(total, axis=0, keepdims=True)
    base = jnp.where(line % 2 == 0, first[0], first[1])
    values = jnp.where(line < 2, values, 2.0 * values - base) * (1.0 / sites)
    spread[...] = jnp.broadcast_to(values[None], spread.shape)
    for k, ref in ((0, odd if STEPS % 2 == 0 else even), (1, even if STEPS % 2 == 0 else odd)):
        for side in (0, 1):
            for m in range(depth):
                ends[k, side, m] = ref[side, m, 16:24, :]


def unturn_kernel(rows, vecs, cols, prev, last, ends, prev_out, last_out, flat, sem):
    depth = prev.shape[0]
    groups = LANES // vecs
    copies = []
    for k, (ref, out) in enumerate(((prev, prev_out), (last, last_out))):
        for m in range(depth):
            for c in range(0, cols, LANES):
                low, high = 8 + c, 8 + c + LANES
                block = []
                if c == 0:
                    block.append(ends[k, 0, m])
                    low += 8
                if c == cols - LANES:
                    high -= 8
                block.append(ref[m, low:high, :])
                if c == cols - LANES:
                    block.append(ends[k, 1, m])
                turned = jnp.concatenate(block, axis=0).T
                for g in range(groups):
                    r = g * depth + m - RIM_R
                    if 0 <= r < rows:
                        flat[k, r, :, c : c + LANES] = turned[g * vecs : (g + 1) * vecs]
            for g in range(groups):
                r = g * depth + m - RIM_R
                if 0 <= r < rows:
                    copy = pltpu.make_async_copy(flat.at[k, r], out.at[:, r, :], sem.at[k, r])
                    copy.start()
                    copies.append(copy)
    for copy in copies:
        copy.wait()


def shift(array, axis, by):
    count = lax.axis_size(axis)
    return lax.ppermute(array, axis, [(i, (i + by) % count) for i in range(count)])


def shape(*dims):
    return jax.ShapeDtypeStruct(dims, F32)


def call(kernel, name, limit, ins, outs, scratch, args, out_specs=None):
    return pl.pallas_call(
        kernel,
        out_shape=outs,
        in_specs=ins,
        out_specs=(VMEM,) * len(outs) if out_specs is None else out_specs,
        scratch_shapes=scratch,
        compiler_params=pltpu.CompilerParams(vmem_limit_bytes=limit << 20),
        name=name,
    )(*args)


def body(vectors, disorder):
    vecs, rows, cols = vectors.shape
    groups = LANES // vecs
    padded = rows + 2 * RIM_R
    depth = padded // groups
    assert vecs * groups == LANES and depth * groups == padded and depth % 2 == 0
    assert rows % 8 == 0 and rows >= 2 * RIM_R and cols % LANES == 0 and cols > 2 * RIM_C
    sites, world = vecs * rows * cols, 1
    for axis in AXES:
        sites *= lax.axis_size(axis)
        world *= lax.axis_size(axis)
    dma = pltpu.SemaphoreType.DMA

    rim = shape(RIM_R * vecs + 8, cols)
    top, bot, vec, dis = call(
        pack_kernel,
        "pack",
        4,
        [HBM, HBM],
        (rim, rim, shape(*vectors.shape), shape(*disorder.shape)),
        [dma((5,))],
        (vectors, disorder),
    )
    lo = shift(bot, "row", 1)
    hi = shift(top, "row", -1)
    wide = cols + 16
    wide += (8 - wide) % 32
    tall = shape(depth, wide, LANES)
    field, edges, dis_turned = call(
        turn_kernel,
        "turn",
        6,
        [VMEM] * 4,
        (tall, shape(2, depth * RIM_C + 8, LANES), shape(cols, LANES)),
        [],
        (lo, hi, vec, dis),
    )
    if lax.axis_size("col") == 2:
        left = right = shift(edges, "col", 1)
        places = (1, 0)
    else:
        left, right = shift(edges[1:], "col", 1), shift(edges[:1], "col", -1)
        places = (0, 0)
    odd, even, partial = call(
        functools.partial(inner_kernel, rows, vecs, cols),
        "inner",
        8,
        [VMEM] * 2,
        (tall, tall, shape(SUMS, 8, LANES)),
        [pltpu.VMEM((depth, cols + 8, LANES), F32)],
        (field, dis_turned),
    )
    strip = pltpu.VMEM((2, depth, 40, LANES), F32)
    ends, spread = call(
        functools.partial(edge_kernel, rows, vecs, cols, places, float(sites)),
        "edge",
        6,
        [VMEM] * 5,
        (shape(2, 2, depth, 8, LANES), shape(world, 1, LANES)),
        [strip, strip, strip, pltpu.VMEM((2, depth, 24, LANES), F32)],
        (field, dis_turned, left, right, partial),
    )
    older, newer = call(
        functools.partial(unturn_kernel, rows, vecs, cols),
        "unturn",
        6,
        [VMEM] * 3,
        (shape(*vectors.shape),) * 2,
        [pltpu.VMEM((2, rows, vecs, cols), F32), dma((2, rows))],
        ((odd, even) if STEPS % 2 == 0 else (even, odd)) + (ends,),
        (HBM, HBM),
    )
    moments = jnp.sum(lax.all_to_all(spread, AXES, 0, 0), axis=0)[0, :SUMS]
    return older, newer, moments


def solution(mesh):
    return jax.shard_map(
        body,
        mesh=mesh,
        in_specs=(P("grp", "row", "col"), P("row", "col")),
        out_specs=(P("grp", "row", "col"), P("grp", "row", "col"), P()),
        check_vma=False,
    )
```

time: 163 us -> 30.2 us (0.19)
  blocking collectives: 40.1 us -> 0 us
  waiting for transfers between devices: 44.3 us -> 7.93 us
  between operations: 19.6 us -> 0.69 us
  other arithmetic: 17.3 us -> 0.05 us
  local copies, waits for them, and re-layouts: 16.7 us -> 2.27 us
  starting transfers between devices: 24.2 us -> 11.2 us
  Pallas kernels: 0 us -> 7.8 us
    ppermute x16 -> x3, waiting for transfers between devices: 44.3 us -> 2.78 us  [shift(): lax.ppermute(array, axis, [(i, (i + by) % count) for i in range(count)])]
    psum x1 -> x0, blocking collectives: 40.1 us -> none  [body(): total_squares = [lax.psum(squares[0], ('grp', 'row', 'col'))]]
    ppermute x16 -> x3, starting transfers between devices: 24.2 us -> 6.72 us  [shift(): lax.ppermute(array, axis, [(i, (i + by) % count) for i in range(count)])]
    another operation x3 -> x0, local copies, waits for them, and re-layouts: 12.8 us -> none  [the longest x1 5.71 us: body(): total_squares = jnp.stack(total_squares)]
    sub x5 -> x0, other arithmetic: 8.54 us -> none  [body(): latest = 2.0 * advance(padded_new) - padded_old[:, 1:-1, 1:-1]]
    pallas_call x0 -> x5, Pallas kernels: none -> 7.8 us  [call(): pl.pallas_call(kernel, out_shape=outs, in_specs=ins, out_specs=(VMEM,) *...]
    all_to_all x0 -> x1, waiting for transfers between devices: none -> 5.15 us  [body(): moments = jnp.sum(lax.all_to_all(spread, AXES, 0, 0), axis=0)[0, :SUMS]]
    all_to_all x0 -> x1, starting transfers between devices: none -> 4.45 us  [body(): moments = jnp.sum(lax.all_to_all(spread, AXES, 0, 0), axis=0)[0, :SUMS]]
  transfers between devices with their start and end apart: 16 -> 4, of which waited for: 8 -> 2; matrix products, arithmetic and copies ran while one was open for 3% -> 0% of each run, Pallas kernels for 0% -> 18%
where the time goes in v2:
time: 30.2 us; the launch traced here: 29.9 us
  starting transfers between devices  11.2 us (37%)
  waiting for transfers between devices  7.93 us (26%)
  Pallas kernels  7.8 us (26%)
  local copies, waits for them, and re-layouts  2.27 us (8%)
  between operations  0.69 us (2%)
    pallas_call x5, Pallas kernels, call(): pl.pallas_call(kernel, out_shape=outs, in_specs=ins, out_specs=(VMEM,) *...  7.8 us
    ppermute x3, starting transfers between devices, shift(): lax.ppermute(array, axis, [(i, (i + by) % count) for i in range(count)])  6.72 us
    all_to_all x1, waiting for transfers between devices, body(): moments = jnp.sum(lax.all_to_all(spread, AXES, 0, 0), axis=0)[0, :SUMS]  5.15 us
    all_to_all x1, starting transfers between devices, body(): moments = jnp.sum(lax.all_to_all(spread, AXES, 0, 0), axis=0)[0, :SUMS]  4.45 us
    ppermute x3, waiting for transfers between devices, shift(): lax.ppermute(array, axis, [(i, (i + by) % count) for i in range(count)])  2.78 us
    unnamed x4, local copies, waits for them, and re-layouts  1.75 us
  transfers between devices with their start and end apart: 4, of which 2 were waited for; matrix products, arithmetic and copies ran while one was open for 0% of the time, Pallas kernels for 18%

profile of v2, /device:TPU:0, one launch (start us, length us, event | category | flops | bytes accessed | tf_op | source)
XLA Modules:
  0.0 29.9 jit_solution(15622862766466148116)
XLA Ops:
  0.6 0.0 copy-start
  0.6 1.0 %copy-done = f32[32,16,256]{2,1,0:T(8,128)S(1)} copy-done((f32[32,16,256]{2,1,0:T(8,128)S(1)}, f32[32,16,256]{2,1,0:T(8,128)}, u32[]{:S(2)}) %copy-start) | copy-done | bytes 524312
  1.7 0.0 copy-start.1
  1.7 0.7 %copy-done.1 = f32[16,256]{1,0:T(8,128)S(1)} copy-done((f32[16,256]{1,0:T(8,128)S(1)}, f32[16,256]{1,0:T(8,128)}, u32[]{:S(2)}) %copy-start.1) | copy-done | bytes 16408
  2.4 0.8 %pack.1 = (f32[136,256]{1,0:T(8,128)S(1)}, f32[136,256]{1,0:T(8,128)S(1)}, f32[32,16,256]{2,1,0:T(8,128)S(1)}, f32[16,256]{1,0:T(8,128)S(1)}) custom-call(f32[32,16,256]{2,1,0:T(8,128)S(1)} %copy-done, f32[16,256]{1,0:T(8,128)S(1)} %copy-done.1), custom_call_target="tpu_custom_call" | custom-call | tf_op jit(solution)/shard_map/pack/pallas_call | solution.py:277
  3.2 0.5 %collective-permute-start = (f32[136,256]{1,0:T(8,128)S(1)}, f32[136,256]{1,0:T(8,128)S(1)}, u32[]{:S(2)}, u32[]{:S(2)}) collective-permute-start(f32[136,256]{1,0:T(8,128)S(1)} %get-tuple-element.17), channel_id=1, source_target_pairs={{0,2},{2,4},{4,6},{6,8},{8,10},{10,12},{12,14},{14,0},{1,3},{3,5},... | collective-permute-start | bytes 417800 | tf_op jit(solution)/shard_map/ppermute | solution.py:269
  3.8 4.1 %collective-permute-start.1 = (f32[136,256]{1,0:T(8,128)S(1)}, f32[136,256]{1,0:T(8,128)S(1)}, u32[]{:S(2)}, u32[]{:S(2)}) collective-permute-start(f32[136,256]{1,0:T(8,128)S(1)} %get-tuple-element.18), channel_id=1, source_target_pairs={{0,14},{2,0},{4,2},{6,4},{8,6},{10,8},{12,10},{14,12},{1,15},{3,1}... | collective-permute-start | bytes 417800 | tf_op jit(solution)/shard_map/ppermute | solution.py:269
  7.9 2.8 %collective-permute-done.lo = f32[136,256]{1,0:T(8,128)S(1)} collective-permute-done((f32[136,256]{1,0:T(8,128)S(1)}, f32[136,256]{1,0:T(8,128)S(1)}, u32[]{:S(2)}, u32[]{:S(2)}) %collective-permute-start) | collective-permute-done | bytes 139296 | tf_op jit(solution)/shard_map/ppermute | solution.py:269
  10.6 0.0 collective-permute-done.1.hi
  10.6 0.3 %turn.1 = (f32[6,296,128]{2,1,0:T(8,128)S(1)}, f32[2,56,128]{2,1,0:T(8,128)S(1)}, f32[256,128]{1,0:T(8,128)S(1)}) custom-call(f32[136,256]{1,0:T(8,128)S(1)} %collective-permute-done.lo, f32[136,256]{1,0:T(8,128)S(1)} %collective-permute-done.1.hi, f32[32,16,256]{2,1,0:T(8,128)S(1)} %get-tuple-element.19.vec, f32[16,256]{1,0:T(8,128)S(1)} %get-tuple-element.20.dis), custom_call_target="tpu_custom_call" | custom-call | tf_op jit(solution)/shard_map/turn/pallas_call | solution.py:277
  11.0 2.1 %collective-permute-start.2 = (f32[2,56,128]{2,1,0:T(8,128)S(1)}, f32[2,56,128]{2,1,0:T(8,128)S(1)}, u32[]{:S(2)}, u32[]{:S(2)}) collective-permute-start(f32[2,56,128]{2,1,0:T(8,128)S(1)} %get-tuple-element.25), channel_id=1, source_target_pairs={{0,1},{1,0},{2,3},{3,2},{4,5},{5,4},{6,7},{7,6},{8,9},{9,8},{10,11... | collective-permute-start | bytes 172040 | tf_op jit(solution)/shard_map/ppermute | solution.py:269
  13.0 3.2 %inner.1 = (f32[6,296,128]{2,1,0:T(8,128)S(1)}, f32[6,296,128]{2,1,0:T(8,128)S(1)}, f32[17,8,128]{2,1,0:T(8,128)S(1)}) custom-call(f32[6,296,128]{2,1,0:T(8,128)S(1)} %get-tuple-element.21.field, f32[256,128]{1,0:T(8,128)S(1)} %get-tuple-element.22.dis_turned), custom_call_target="tpu_custom_call" | custom-call | tf_op jit(solution)/shard_map/inner/pallas_call | solution.py:277
  16.3 0.0 collective-permute-done.2.left.right
  16.3 1.3 %edge.1 = (f32[2,2,6,8,128]{4,3,2,1,0:T(8,128)S(1)}, f32[32,1,128]{2,1,0:T(1,128)}) custom-call(f32[6,296,128]{2,1,0:T(8,128)S(1)} %get-tuple-element.21.field, f32[256,128]{1,0:T(8,128)S(1)} %get-tuple-element.22.dis_turned, f32[2,56,128]{2,1,0:T(8,128)S(1)} %collective-permute-done.2.left.right, f32[2,56,128]{2,1,0:T(8,128)S(1)} %collective-permute-done.2.left.right, ...), custom_call_target="tpu_custom_call" | custom-call | tf_op jit(solution)/shard_map/edge/pallas_call | solution.py:277
  17.6 4.5 %all-to-all-start = ((f32[32,1,128]{2,1,0:T(1,128)}), f32[32,1,128]{2,1,0:T(1,128)S(1)}, u32[]{:S(2)}, u32[]{:S(2)}) async-start(f32[32,1,128]{2,1,0:T(1,128)} %get-tuple-element.30), calls=%async_computation | async-start | bytes 32768 | tf_op jit(solution)/shard_map/all_to_all | solution.py:360
  22.1 2.1 %unturn.1 = (f32[32,16,256]{2,1,0:T(8,128)}, f32[32,16,256]{2,1,0:T(8,128)}) custom-call(f32[6,296,128]{2,1,0:T(8,128)S(1)} %get-tuple-element.23.prev, f32[6,296,128]{2,1,0:T(8,128)S(1)} %get-tuple-element.24.last, f32[2,2,6,8,128]{4,3,2,1,0:T(8,128)S(1)} %get-tuple-element.27.ends), custom_call_target="tpu_custom_call" | custom-call | tf_op jit(solution)/shard_map/unturn/pallas_call | solution.py:277
  24.2 5.2 %all-to-all-done = f32[32,1,128]{2,1,0:T(1,128)S(1)} async-done(((f32[32,1,128]{2,1,0:T(1,128)}), f32[32,1,128]{2,1,0:T(1,128)S(1)}, u32[]{:S(2)}, u32[]{:S(2)}) %all-to-all-start) | async-done | bytes 16416 | tf_op jit(solution)/shard_map/all_to_all | solution.py:360
  29.3 0.1 reduce_sum.11
  29.4 0.5 %slice_bitcast_fusion = f32[17]{0:T(128)} fusion(f32[1,128]{1,0:T(1,128)S(1)} %bitcast.3), kind=kLoop, calls=%fused_computation | loop fusion | bytes 136 | tf_op jit(solution)/shard_map/squeeze | solution.py:360
Async XLA Ops:
  0.6 1.0 %copy-start = (f32[32,16,256]{2,1,0:T(8,128)S(1)}, f32[32,16,256]{2,1,0:T(8,128)}, u32[]{:S(2)}) copy-start(f32[32,16,256]{2,1,0:T(8,128)} %vec.1) | copy-start | bytes 1572868
  1.7 0.7 %copy-start.1 = (f32[16,256]{1,0:T(8,128)S(1)}, f32[16,256]{1,0:T(8,128)}, u32[]{:S(2)}) copy-start(f32[16,256]{1,0:T(8,128)} %dis.1) | copy-start | bytes 49156
  3.2 7.4 %collective-permute-start = (f32[136,256]{1,0:T(8,128)S(1)}, f32[136,256]{1,0:T(8,128)S(1)}, u32[]{:S(2)}, u32[]{:S(2)}) collective-permute-start(f32[136,256]{1,0:T(8,128)S(1)} %get-tuple-element.17), channel_id=1, source_target_pairs={{0,2},{2,4},{4,6},{6,8},{8,10},{10,12},{12,14},{14,0},{1,3},{3,5},... | collective-permute-start | bytes 417800 | tf_op jit(solution)/shard_map/ppermute | solution.py:269
  3.8 6.9 %collective-permute-start.1 = (f32[136,256]{1,0:T(8,128)S(1)}, f32[136,256]{1,0:T(8,128)S(1)}, u32[]{:S(2)}, u32[]{:S(2)}) collective-permute-start(f32[136,256]{1,0:T(8,128)S(1)} %get-tuple-element.18), channel_id=1, source_target_pairs={{0,14},{2,0},{4,2},{6,4},{8,6},{10,8},{12,10},{14,12},{1,15},{3,1}... | collective-permute-start | bytes 417800 | tf_op jit(solution)/shard_map/ppermute | solution.py:269
  11.0 5.3 %collective-permute-start.2 = (f32[2,56,128]{2,1,0:T(8,128)S(1)}, f32[2,56,128]{2,1,0:T(8,128)S(1)}, u32[]{:S(2)}, u32[]{:S(2)}) collective-permute-start(f32[2,56,128]{2,1,0:T(8,128)S(1)} %get-tuple-element.25), channel_id=1, source_target_pairs={{0,1},{1,0},{2,3},{3,2},{4,5},{5,4},{6,7},{7,6},{8,9},{9,8},{10,11... | collective-permute-start | bytes 172040 | tf_op jit(solution)/shard_map/ppermute | solution.py:269
  17.6 11.7 %all-to-all-start = ((f32[32,1,128]{2,1,0:T(1,128)}), f32[32,1,128]{2,1,0:T(1,128)S(1)}, u32[]{:S(2)}, u32[]{:S(2)}) async-start(f32[32,1,128]{2,1,0:T(1,128)} %get-tuple-element.30), calls=%async_computation | async-start | bytes 32768 | tf_op jit(solution)/shard_map/all_to_all | solution.py:360

commit v3 on v2

--- a/solution.py
+++ b/solution.py
@@ -306,7 +306,10 @@
         [HBM, HBM],
         (rim, rim, shape(*vectors.shape), shape(*disorder.shape)),
         [dma((5,))],
-        (vectors, disorder),
+        (
+            pltpu.with_memory_space_constraint(vectors, pltpu.HBM),
+            pltpu.with_memory_space_constraint(disorder, pltpu.HBM),
+        ),
     )
     lo = shift(bot, "row", 1)
     hi = shift(top, "row", -1)
@@ -343,7 +346,7 @@
         "edge",
         6,
         [VMEM] * 5,
-        (shape(2, 2, depth, 8, LANES), shape(world, 1, LANES)),
+        (shape(2, 2, depth, 8, LANES), pltpu.VMEM((world, 1, LANES), F32)),
         [strip, strip, strip, pltpu.VMEM((2, depth, 24, LANES), F32)],
         (field, dis_turned, left, right, partial),
     )

time: 30.2 us -> 28.8 us (0.954)
  local copies, waits for them, and re-layouts: 2.27 us -> 0.51 us
  Pallas kernels: 7.8 us -> 8.16 us
    unnamed x4 -> x0, local copies, waits for them, and re-layouts: 1.75 us -> none
    pallas_call x5, Pallas kernels: 7.8 us -> 8.16 us  [call(): pl.pallas_call(kernel, out_shape=outs, in_specs=ins, out_specs=(VMEM,) *...]
  transfers between devices with their start and end apart: 4 -> 4, of which waited for: 2 -> 2; matrix products, arithmetic and copies ran while one was open for 0% -> 0% of each run, Pallas kernels for 18% -> 19%
where the time goes in v3:
time: 28.8 us; the launch traced here: 28.5 us
  starting transfers between devices  11.2 us (39%)
  Pallas kernels  8.16 us (28%)
  waiting for transfers between devices  7.92 us (28%)
  between operations  0.68 us (2%)
  local copies, waits for them, and re-layouts  0.51 us (2%)
    pallas_call x5, Pallas kernels, call(): pl.pallas_call(kernel, out_shape=outs, in_specs=ins, out_specs=(VMEM,) *...  8.16 us
    ppermute x3, starting transfers between devices, shift(): lax.ppermute(array, axis, [(i, (i + by) % count) for i in range(count)])  6.72 us
    all_to_all x1, waiting for transfers between devices, body(): moments = jnp.sum(lax.all_to_all(spread, AXES, 0, 0), axis=0)[0, :SUMS]  5.15 us
    all_to_all x1, starting transfers between devices, body(): moments = jnp.sum(lax.all_to_all(spread, AXES, 0, 0), axis=0)[0, :SUMS]  4.45 us
    ppermute x3, waiting for transfers between devices, shift(): lax.ppermute(array, axis, [(i, (i + by) % count) for i in range(count)])  2.78 us
  transfers between devices with their start and end apart: 4, of which 2 were waited for; matrix products, arithmetic and copies ran while one was open for 0% of the time, Pallas kernels for 19%

profile of v3, /device:TPU:0, one launch (start us, length us, event | category | flops | bytes accessed | tf_op | source)
XLA Modules:
  0.0 28.5 jit_solution(4998442427622391936)
XLA Ops:
  0.6 1.2 %pack.1 = (f32[136,256]{1,0:T(8,128)S(1)}, f32[136,256]{1,0:T(8,128)S(1)}, f32[32,16,256]{2,1,0:T(8,128)S(1)}, f32[16,256]{1,0:T(8,128)S(1)}) custom-call(f32[32,16,256]{2,1,0:T(8,128)} %vec.1, f32[16,256]{1,0:T(8,128)} %dis.1), custom_call_target="tpu_custom_call" | custom-call | tf_op jit(solution)/shard_map/pack/pallas_call | solution.py:277
  1.8 0.5 %collective-permute-start = (f32[136,256]{1,0:T(8,128)S(1)}, f32[136,256]{1,0:T(8,128)S(1)}, u32[]{:S(2)}, u32[]{:S(2)}) collective-permute-start(f32[136,256]{1,0:T(8,128)S(1)} %get-tuple-element.17), channel_id=1, source_target_pairs={{0,2},{2,4},{4,6},{6,8},{8,10},{10,12},{12,14},{14,0},{1,3},{3,5},... | collective-permute-start | bytes 417800 | tf_op jit(solution)/shard_map/ppermute | solution.py:269
  2.4 4.1 %collective-permute-start.1 = (f32[136,256]{1,0:T(8,128)S(1)}, f32[136,256]{1,0:T(8,128)S(1)}, u32[]{:S(2)}, u32[]{:S(2)}) collective-permute-start(f32[136,256]{1,0:T(8,128)S(1)} %get-tuple-element.18), channel_id=1, source_target_pairs={{0,14},{2,0},{4,2},{6,4},{8,6},{10,8},{12,10},{14,12},{1,15},{3,1}... | collective-permute-start | bytes 417800 | tf_op jit(solution)/shard_map/ppermute | solution.py:269
  6.5 2.8 %collective-permute-done.lo = f32[136,256]{1,0:T(8,128)S(1)} collective-permute-done((f32[136,256]{1,0:T(8,128)S(1)}, f32[136,256]{1,0:T(8,128)S(1)}, u32[]{:S(2)}, u32[]{:S(2)}) %collective-permute-start) | collective-permute-done | bytes 139296 | tf_op jit(solution)/shard_map/ppermute | solution.py:269
  9.2 0.0 collective-permute-done.1.hi
  9.2 0.3 %turn.1 = (f32[6,296,128]{2,1,0:T(8,128)S(1)}, f32[2,56,128]{2,1,0:T(8,128)S(1)}, f32[256,128]{1,0:T(8,128)S(1)}) custom-call(f32[136,256]{1,0:T(8,128)S(1)} %collective-permute-done.lo, f32[136,256]{1,0:T(8,128)S(1)} %collective-permute-done.1.hi, f32[32,16,256]{2,1,0:T(8,128)S(1)} %get-tuple-element.19.vec, f32[16,256]{1,0:T(8,128)S(1)} %get-tuple-element.20.dis), custom_call_target="tpu_custom_call" | custom-call | tf_op jit(solution)/shard_map/turn/pallas_call | solution.py:277
  9.6 2.1 %collective-permute-start.2 = (f32[2,56,128]{2,1,0:T(8,128)S(1)}, f32[2,56,128]{2,1,0:T(8,128)S(1)}, u32[]{:S(2)}, u32[]{:S(2)}) collective-permute-start(f32[2,56,128]{2,1,0:T(8,128)S(1)} %get-tuple-element.25), channel_id=1, source_target_pairs={{0,1},{1,0},{2,3},{3,2},{4,5},{5,4},{6,7},{7,6},{8,9},{9,8},{10,11... | collective-permute-start | bytes 172040 | tf_op jit(solution)/shard_map/ppermute | solution.py:269
  11.6 3.2 %inner.1 = (f32[6,296,128]{2,1,0:T(8,128)S(1)}, f32[6,296,128]{2,1,0:T(8,128)S(1)}, f32[17,8,128]{2,1,0:T(8,128)S(1)}) custom-call(f32[6,296,128]{2,1,0:T(8,128)S(1)} %get-tuple-element.21.field, f32[256,128]{1,0:T(8,128)S(1)} %get-tuple-element.22.dis_turned), custom_call_target="tpu_custom_call" | custom-call | tf_op jit(solution)/shard_map/inner/pallas_call | solution.py:277
  14.9 0.0 collective-permute-done.2.left.right
  14.9 1.3 %edge.1 = (f32[2,2,6,8,128]{4,3,2,1,0:T(8,128)S(1)}, f32[32,1,128]{2,1,0:T(1,128)}) custom-call(f32[6,296,128]{2,1,0:T(8,128)S(1)} %get-tuple-element.21.field, f32[256,128]{1,0:T(8,128)S(1)} %get-tuple-element.22.dis_turned, f32[2,56,128]{2,1,0:T(8,128)S(1)} %collective-permute-done.2.left.right, f32[2,56,128]{2,1,0:T(8,128)S(1)} %collective-permute-done.2.left.right, ...), custom_call_target="tpu_custom_call" | custom-call | tf_op jit(solution)/shard_map/edge/pallas_call | solution.py:277
  16.2 4.5 %all-to-all-start = ((f32[32,1,128]{2,1,0:T(1,128)}), f32[32,1,128]{2,1,0:T(1,128)S(1)}, u32[]{:S(2)}, u32[]{:S(2)}) async-start(f32[32,1,128]{2,1,0:T(1,128)} %get-tuple-element.30), calls=%async_computation | async-start | bytes 32768 | tf_op jit(solution)/shard_map/all_to_all | solution.py:363
  20.7 2.1 %unturn.1 = (f32[32,16,256]{2,1,0:T(8,128)}, f32[32,16,256]{2,1,0:T(8,128)}) custom-call(f32[6,296,128]{2,1,0:T(8,128)S(1)} %get-tuple-element.23.prev, f32[6,296,128]{2,1,0:T(8,128)S(1)} %get-tuple-element.24.last, f32[2,2,6,8,128]{4,3,2,1,0:T(8,128)S(1)} %get-tuple-element.27.ends), custom_call_target="tpu_custom_call" | custom-call | tf_op jit(solution)/shard_map/unturn/pallas_call | solution.py:277
  22.8 5.1 %all-to-all-done = f32[32,1,128]{2,1,0:T(1,128)S(1)} async-done(((f32[32,1,128]{2,1,0:T(1,128)}), f32[32,1,128]{2,1,0:T(1,128)S(1)}, u32[]{:S(2)}, u32[]{:S(2)}) %all-to-all-start) | async-done | bytes 16416 | tf_op jit(solution)/shard_map/all_to_all | solution.py:363
  27.9 0.1 reduce_sum.11
  28.0 0.5 %slice_bitcast_fusion = f32[17]{0:T(128)} fusion(f32[1,128]{1,0:T(1,128)S(1)} %bitcast.3), kind=kLoop, calls=%fused_computation | loop fusion | bytes 136 | tf_op jit(solution)/shard_map/squeeze | solution.py:363
Async XLA Ops:
  1.8 7.4 %collective-permute-start = (f32[136,256]{1,0:T(8,128)S(1)}, f32[136,256]{1,0:T(8,128)S(1)}, u32[]{:S(2)}, u32[]{:S(2)}) collective-permute-start(f32[136,256]{1,0:T(8,128)S(1)} %get-tuple-element.17), channel_id=1, source_target_pairs={{0,2},{2,4},{4,6},{6,8},{8,10},{10,12},{12,14},{14,0},{1,3},{3,5},... | collective-permute-start | bytes 417800 | tf_op jit(solution)/shard_map/ppermute | solution.py:269
  2.4 6.9 %collective-permute-start.1 = (f32[136,256]{1,0:T(8,128)S(1)}, f32[136,256]{1,0:T(8,128)S(1)}, u32[]{:S(2)}, u32[]{:S(2)}) collective-permute-start(f32[136,256]{1,0:T(8,128)S(1)} %get-tuple-element.18), channel_id=1, source_target_pairs={{0,14},{2,0},{4,2},{6,4},{8,6},{10,8},{12,10},{14,12},{1,15},{3,1}... | collective-permute-start | bytes 417800 | tf_op jit(solution)/shard_map/ppermute | solution.py:269
  9.6 5.3 %collective-permute-start.2 = (f32[2,56,128]{2,1,0:T(8,128)S(1)}, f32[2,56,128]{2,1,0:T(8,128)S(1)}, u32[]{:S(2)}, u32[]{:S(2)}) collective-permute-start(f32[2,56,128]{2,1,0:T(8,128)S(1)} %get-tuple-element.25), channel_id=1, source_target_pairs={{0,1},{1,0},{2,3},{3,2},{4,5},{5,4},{6,7},{7,6},{8,9},{9,8},{10,11... | collective-permute-start | bytes 172040 | tf_op jit(solution)/shard_map/ppermute | solution.py:269
  16.2 11.7 %all-to-all-start = ((f32[32,1,128]{2,1,0:T(1,128)}), f32[32,1,128]{2,1,0:T(1,128)S(1)}, u32[]{:S(2)}, u32[]{:S(2)}) async-start(f32[32,1,128]{2,1,0:T(1,128)} %get-tuple-element.30), calls=%async_computation | async-start | bytes 32768 | tf_op jit(solution)/shard_map/all_to_all | solution.py:363

commit v4 on v2

--- a/solution.py
+++ b/solution.py
@@ -20,25 +20,28 @@
 F32 = jnp.float32
 
 
-def pack_kernel(vec, dis, top, bot, vec_out, dis_out, sem):
+def pack_kernel(vec, dis, top, bot, sem):
     vecs, rows, _ = vec.shape
-    parts = 4
-    some = vecs // parts
-    copies = [pltpu.make_async_copy(dis, dis_out, sem.at[parts])]
-    for k in range(parts):
-        here = pl.ds(k * some, some)
-        copies.append(pltpu.make_async_copy(vec.at[here], vec_out.at[here], sem.at[k]))
+    copies = []
+    for k, (out, first) in enumerate(((top, 0), (bot, rows - RIM_R))):
+        place = pl.ds(first, RIM_R)
+        copies.append(pltpu.make_async_copy(vec.at[:, place, :], out.at[pl.ds(0, vecs)], sem.at[k, 0]))
+        copies.append(pltpu.make_async_copy(dis.at[place, :], out.at[vecs], sem.at[k, 1]))
     for copy in copies:
         copy.start()
-    copies[0].wait()
-    top[RIM_R * vecs :, :] = dis_out[:8, :]
-    bot[RIM_R * vecs :, :] = dis_out[rows - 8 :, :]
-    for k in range(parts):
-        copies[1 + k].wait()
-        for r in range(RIM_R):
-            line = r * vecs + k * some
-            top[line : line + some, :] = vec_out[k * some : (k + 1) * some, r, :]
-            bot[line : line + some, :] = vec_out[k * some : (k + 1) * some, rows - RIM_R + r, :]
+    for copy in copies:
+        copy.wait()
+
+
+def load_kernel(after, vec, dis, vec_out, dis_out, sem):
+    copies = [
+        pltpu.make_async_copy(vec, vec_out, sem.at[0]),
+        pltpu.make_async_copy(dis, dis_out, sem.at[1]),
+    ]
+    for copy in copies:
+        copy.start()
+    for copy in copies:
+        copy.wait()
 
 
 def turn_kernel(lo, hi, vec, dis, field, edges, dis_turned):
@@ -46,15 +49,13 @@
     groups = LANES // vecs
     padded = rows + 2 * RIM_R
     depth = padded // groups
-    at = RIM_R * vecs
 
     def lines(p, c):
         if p < RIM_R:
-            return lo[p * vecs : (p + 1) * vecs, c : c + LANES]
+            return lo[:vecs, p, c : c + LANES]
         if p < RIM_R + rows:
             return vec[:, p - RIM_R, c : c + LANES]
-        p -= RIM_R + rows
-        return hi[p * vecs : (p + 1) * vecs, c : c + LANES]
+        return hi[:vecs, p - RIM_R - rows, c : c + LANES]
 
     ends = ((0, 0), (cols - LANES, LANES - RIM_C))
     for c in range(0, cols, LANES):
@@ -65,9 +66,9 @@
                 if c == place:
                     edges[side, m * RIM_C : (m + 1) * RIM_C, :] = turned[first : first + RIM_C]
         block = [
-            lo[at + 8 - RIM_R : at + 8, c : c + LANES],
+            lo[vecs, :, c : c + LANES],
             dis[:, c : c + LANES],
-            hi[at : at + RIM_R, c : c + LANES],
+            hi[vecs, :, c : c + LANES],
             jnp.zeros((LANES - padded, LANES), F32),
         ]
         turned = jnp.concatenate(block, axis=0).T * (2.0 / SCALE)
@@ -232,7 +233,11 @@
                 ends[k, side, m] = ref[side, m, 16:24, :]
 
 
-def unturn_kernel(rows, vecs, cols, prev, last, ends, prev_out, last_out, flat, sem):
+def on_first_chip():
+    return (lax.axis_index("grp") == 0) & (lax.axis_index("row") < 2) & (lax.axis_index("col") == 0)
+
+
+def unturn(rows, vecs, cols, prev, last, ends, prev_out, last_out, flat, sem):
     depth = prev.shape[0]
     groups = LANES // vecs
     copies = []
@@ -253,15 +258,28 @@
                 for g in range(groups):
                     r = g * depth + m - RIM_R
                     if 0 <= r < rows:
-                        flat[k, r, :, c : c + LANES] = turned[g * vecs : (g + 1) * vecs]
-            for g in range(groups):
-                r = g * depth + m - RIM_R
-                if 0 <= r < rows:
-                    copy = pltpu.make_async_copy(flat.at[k, r], out.at[:, r, :], sem.at[k, r])
-                    copy.start()
-                    copies.append(copy)
+                        flat[k, :, r, c : c + LANES] = turned[g * vecs : (g + 1) * vecs]
+        copy = pltpu.make_async_copy(flat.at[k], out, sem.at[k])
+        copy.start()
+        copies.append(copy)
     for copy in copies:
         copy.wait()
+
+
+def before_kernel(rows, vecs, cols, prev, last, ends, spread, prev_out, last_out, spread_out, flat, sem):
+    spread_out[...] = spread[...]
+
+    @pl.when(on_first_chip())
+    def _():
+        unturn(rows, vecs, cols, prev, last, ends, prev_out, last_out, flat, sem)
+
+
+def after_kernel(rows, vecs, cols, sums, prev, last, ends, prev_in, last_in, prev_out, last_out, moments, flat, sem):
+    moments[...] = jnp.sum(sums[...], axis=0)[:, :SUMS]
+
+    @pl.when(jnp.logical_not(on_first_chip()))
+    def _():
+        unturn(rows, vecs, cols, prev, last, ends, prev_out, last_out, flat, sem)
 
 
 def shift(array, axis, by):
@@ -273,13 +291,14 @@
     return jax.ShapeDtypeStruct(dims, F32)
 
 
-def call(kernel, name, limit, ins, outs, scratch, args, out_specs=None):
+def call(kernel, name, limit, ins, outs, scratch, args, out_specs=None, aliases={}):
     return pl.pallas_call(
         kernel,
         out_shape=outs,
         in_specs=ins,
         out_specs=(VMEM,) * len(outs) if out_specs is None else out_specs,
         scratch_shapes=scratch,
+        input_output_aliases=aliases,
         compiler_params=pltpu.CompilerParams(vmem_limit_bytes=limit << 20),
         name=name,
     )(*args)
@@ -298,15 +317,20 @@
         world *= lax.axis_size(axis)
     dma = pltpu.SemaphoreType.DMA
 
-    rim = shape(RIM_R * vecs + 8, cols)
-    top, bot, vec, dis = call(
-        pack_kernel,
-        "pack",
-        4,
-        [HBM, HBM],
-        (rim, rim, shape(*vectors.shape), shape(*disorder.shape)),
-        [dma((5,))],
-        (vectors, disorder),
+    rim = shape(vecs + 1, RIM_R, cols)
+    inputs = (
+        pltpu.with_memory_space_constraint(vectors, pltpu.HBM),
+        pltpu.with_memory_space_constraint(disorder, pltpu.HBM),
+    )
+    top, bot = call(pack_kernel, "pack", 2, [HBM, HBM], (rim, rim), [dma((2, 2))], inputs)
+    vec, dis = call(
+        load_kernel,
+        "load",
+        2,
+        [VMEM, HBM, HBM],
+        (shape(*vectors.shape), shape(*disorder.shape)),
+        [dma((2,))],
+        (top,) + inputs,
     )
     lo = shift(bot, "row", 1)
     hi = shift(top, "row", -1)
@@ -347,18 +371,32 @@
         [strip, strip, strip, pltpu.VMEM((2, depth, 24, LANES), F32)],
         (field, dis_turned, left, right, partial),
     )
-    older, newer = call(
-        functools.partial(unturn_kernel, rows, vecs, cols),
-        "unturn",
+    fields = ((odd, even) if STEPS % 2 == 0 else (even, odd)) + (ends,)
+    whole = (shape(*vectors.shape),) * 2
+    scratch = [pltpu.VMEM((2, vecs, rows, cols), F32), dma((2,))]
+    older, newer, spread = call(
+        functools.partial(before_kernel, rows, vecs, cols),
+        "before",
         6,
-        [VMEM] * 3,
-        (shape(*vectors.shape),) * 2,
-        [pltpu.VMEM((2, rows, vecs, cols), F32), dma((2, rows))],
-        ((odd, even) if STEPS % 2 == 0 else (even, odd)) + (ends,),
-        (HBM, HBM),
-    )
-    moments = jnp.sum(lax.all_to_all(spread, AXES, 0, 0), axis=0)[0, :SUMS]
-    return older, newer, moments
+        [VMEM] * 4,
+        whole + (shape(world, 1, LANES),),
+        scratch,
+        fields + (spread,),
+        (HBM, HBM, VMEM),
+    )
+    sums = lax.all_to_all(spread, AXES, 0, 0)
+    older, newer, moments = call(
+        functools.partial(after_kernel, rows, vecs, cols),
+        "after",
+        6,
+        [VMEM] * 4 + [HBM] * 2,
+        whole + (shape(1, SUMS),),
+        scratch,
+        (sums,) + fields + (older, newer),
+        (HBM, HBM, VMEM),
+        {4: 0, 5: 1},
+    )
+    return older, newer, moments[0]
 
 
 def solution(mesh):

time: 30.2 us -> 28 us (0.927)
  blocking collectives: 0 us -> 9.97 us
  waiting for transfers between devices: 7.93 us -> 1.66 us
  starting transfers between devices: 11.2 us -> 6.72 us
  local copies, waits for them, and re-layouts: 2.27 us -> 0 us
  Pallas kernels: 7.8 us -> 8.74 us
    all_to_all x0 -> x1, blocking collectives: none -> 9.97 us  [body(): sums = lax.all_to_all(spread, AXES, 0, 0)]
    all_to_all x1 -> x0, waiting for transfers between devices: 5.15 us -> none  [body(): moments = jnp.sum(lax.all_to_all(spread, AXES, 0, 0), axis=0)[0, :SUMS]]
    all_to_all x1 -> x0, starting transfers between devices: 4.45 us -> none  [body(): moments = jnp.sum(lax.all_to_all(spread, AXES, 0, 0), axis=0)[0, :SUMS]]
    unnamed x4 -> x0, local copies, waits for them, and re-layouts: 1.75 us -> none
    ppermute x3, waiting for transfers between devices: 2.78 us -> 1.66 us  [shift(): lax.ppermute(array, axis, [(i, (i + by) % count) for i in range(count)])]
    pallas_call x5 -> x7, Pallas kernels: 7.8 us -> 8.74 us  [call(): pl.pallas_call(kernel, out_shape=outs, in_specs=ins, out_specs=(VMEM,) *...]
    squeeze x1 -> x0, local copies, waits for them, and re-layouts: 0.51 us -> none  [body(): moments = jnp.sum(lax.all_to_all(spread, AXES, 0, 0), axis=0)[0, :SUMS]]
  transfers between devices with their start and end apart: 4 -> 3, of which waited for: 2 -> 1; matrix products, arithmetic and copies ran while one was open for 0% -> 0% of each run, Pallas kernels for 18% -> 16%
where the time goes in v4:
time: 28 us; the launch traced here: 27.8 us
  blocking collectives  9.97 us (36%)
  Pallas kernels  8.74 us (31%)
  starting transfers between devices  6.72 us (24%)
  waiting for transfers between devices  1.66 us (6%)
  between operations  0.68 us (2%)
    all_to_all x1, blocking collectives, body(): sums = lax.all_to_all(spread, AXES, 0, 0)  9.97 us
    pallas_call x7, Pallas kernels, call(): pl.pallas_call(kernel, out_shape=outs, in_specs=ins, out_specs=(VMEM,) *...  8.74 us
    ppermute x3, starting transfers between devices, shift(): lax.ppermute(array, axis, [(i, (i + by) % count) for i in range(count)])  6.72 us
    ppermute x3, waiting for transfers between devices, shift(): lax.ppermute(array, axis, [(i, (i + by) % count) for i in range(count)])  1.66 us
  transfers between devices with their start and end apart: 3, of which 1 were waited for; matrix products, arithmetic and copies ran while one was open for 0% of the time, Pallas kernels for 16%

profile of v4, /device:TPU:0, one launch (start us, length us, event | category | flops | bytes accessed | tf_op | source)
XLA Modules:
  0.0 27.8 jit_solution(5000072935943739931)
XLA Ops:
  0.6 1.0 %pack.1 = (f32[33,4,256]{2,1,0:T(4,128)S(1)}, f32[33,4,256]{2,1,0:T(4,128)S(1)}) custom-call(f32[32,16,256]{2,1,0:T(8,128)} %vec.3, f32[16,256]{1,0:T(8,128)} %dis.3), custom_call_target="tpu_custom_call" | custom-call | tf_op jit(solution)/shard_map/pack/pallas_call | solution.py:295
  1.7 0.5 %collective-permute-start = (f32[33,4,256]{2,1,0:T(4,128)S(1)}, f32[33,4,256]{2,1,0:T(4,128)S(1)}, u32[]{:S(2)}, u32[]{:S(2)}) collective-permute-start(f32[33,4,256]{2,1,0:T(4,128)S(1)} %get-tuple-element.21), channel_id=1, source_target_pairs={{0,2},{2,4},{4,6},{6,8},{8,10},{10,12},{12,14},{14,0},{1,3},{3,5},... | collective-permute-start | bytes 405512 | tf_op jit(solution)/shard_map/ppermute | solution.py:287
  2.2 4.1 %collective-permute-start.1 = (f32[33,4,256]{2,1,0:T(4,128)S(1)}, f32[33,4,256]{2,1,0:T(4,128)S(1)}, u32[]{:S(2)}, u32[]{:S(2)}) collective-permute-start(f32[33,4,256]{2,1,0:T(4,128)S(1)} %get-tuple-element.22.after), channel_id=1, source_target_pairs={{0,14},{2,0},{4,2},{6,4},{8,6},{10,8},{12,10},{14,12},{1,15},{3,1}... | collective-permute-start | bytes 405512 | tf_op jit(solution)/shard_map/ppermute | solution.py:287
  6.3 1.1 %load.1 = (f32[32,16,256]{2,1,0:T(8,128)S(1)}, f32[16,256]{1,0:T(8,128)S(1)}) custom-call(f32[33,4,256]{2,1,0:T(4,128)S(1)} %get-tuple-element.22.after, f32[32,16,256]{2,1,0:T(8,128)} %vec.3, f32[16,256]{1,0:T(8,128)} %dis.3), custom_call_target="tpu_custom_call" | custom-call | tf_op jit(solution)/shard_map/load/pallas_call | solution.py:295
  7.4 1.7 %collective-permute-done.lo = f32[33,4,256]{2,1,0:T(4,128)S(1)} collective-permute-done((f32[33,4,256]{2,1,0:T(4,128)S(1)}, f32[33,4,256]{2,1,0:T(4,128)S(1)}, u32[]{:S(2)}, u32[]{:S(2)}) %collective-permute-start) | collective-permute-done | bytes 135200 | tf_op jit(solution)/shard_map/ppermute | solution.py:287
  9.0 0.0 collective-permute-done.1.hi
  9.0 0.4 %turn.1 = (f32[6,296,128]{2,1,0:T(8,128)S(1)}, f32[2,56,128]{2,1,0:T(8,128)S(1)}, f32[256,128]{1,0:T(8,128)S(1)}) custom-call(f32[33,4,256]{2,1,0:T(4,128)S(1)} %collective-permute-done.lo, f32[33,4,256]{2,1,0:T(4,128)S(1)} %collective-permute-done.1.hi, f32[32,16,256]{2,1,0:T(8,128)S(1)} %get-tuple-element.23.vec, f32[16,256]{1,0:T(8,128)S(1)} %get-tuple-element.24.dis), custom_call_target="tpu_custom_call" | custom-call | tf_op jit(solution)/shard_map/turn/pallas_call | solution.py:295
  9.5 2.1 %collective-permute-start.2 = (f32[2,56,128]{2,1,0:T(8,128)S(1)}, f32[2,56,128]{2,1,0:T(8,128)S(1)}, u32[]{:S(2)}, u32[]{:S(2)}) collective-permute-start(f32[2,56,128]{2,1,0:T(8,128)S(1)} %get-tuple-element.29), channel_id=1, source_target_pairs={{0,1},{1,0},{2,3},{3,2},{4,5},{5,4},{6,7},{7,6},{8,9},{9,8},{10,11... | collective-permute-start | bytes 172040 | tf_op jit(solution)/shard_map/ppermute | solution.py:287
  11.6 3.4 %inner.1 = (f32[6,296,128]{2,1,0:T(8,128)S(1)}, f32[6,296,128]{2,1,0:T(8,128)S(1)}, f32[17,8,128]{2,1,0:T(8,128)S(1)}) custom-call(f32[6,296,128]{2,1,0:T(8,128)S(1)} %get-tuple-element.25.field, f32[256,128]{1,0:T(8,128)S(1)} %get-tuple-element.26.dis_turned), custom_call_target="tpu_custom_call" | custom-call | tf_op jit(solution)/shard_map/inner/pallas_call | solution.py:295
  14.9 0.0 collective-permute-done.2.left.right
  14.9 0.7 %edge.1 = (f32[2,2,6,8,128]{4,3,2,1,0:T(8,128)S(1)}, f32[32,1,128]{2,1,0:T(1,128)S(1)}) custom-call(f32[6,296,128]{2,1,0:T(8,128)S(1)} %get-tuple-element.25.field, f32[256,128]{1,0:T(8,128)S(1)} %get-tuple-element.26.dis_turned, f32[2,56,128]{2,1,0:T(8,128)S(1)} %collective-permute-done.2.left.right, f32[2,56,128]{2,1,0:T(8,128)S(1)} %collective-permute-done.2.left.right, ...), custom_call_target="tpu_custom_call" | custom-call | tf_op jit(solution)/shard_map/edge/pallas_call | solution.py:295
  15.7 1.6 %before.1 = (f32[32,16,256]{2,1,0:T(8,128)}, f32[32,16,256]{2,1,0:T(8,128)}, f32[32,1,128]{2,1,0:T(1,128)S(1)}) custom-call(f32[6,296,128]{2,1,0:T(8,128)S(1)} %get-tuple-element.27.prev, f32[6,296,128]{2,1,0:T(8,128)S(1)} %get-tuple-element.28.last, f32[2,2,6,8,128]{4,3,2,1,0:T(8,128)S(1)} %get-tuple-element.31.ends, f32[32,1,128]{2,1,0:T(1,128)S(1)} %get-tuple-element.32.spread), custom_call_target="tpu_custom_call" | custom-call | tf_op jit(solution)/shard_map/before/pallas_call | solution.py:295
  17.2 10.0 %all_to_all.5.sums = f32[32,1,128]{2,1,0:T(1,128)S(1)} all-to-all(f32[32,1,128]{2,1,0:T(1,128)S(1)} %get-tuple-element.33), channel_id=1, replica_groups=mesh['grp'=2,'row'=8,'col'=2] {'grp','row','col'}, dimensions={0} | all-to-all | bytes 32768 | tf_op jit(solution)/shard_map/all_to_all | solution.py:387
  27.2 0.6 %after.1 = (f32[32,16,256]{2,1,0:T(8,128)}, f32[32,16,256]{2,1,0:T(8,128)}, f32[1,17]{1,0:T(1,128)}) custom-call(f32[32,1,128]{2,1,0:T(1,128)S(1)} %all_to_all.5.sums, f32[6,296,128]{2,1,0:T(8,128)S(1)} %get-tuple-element.27.prev, f32[6,296,128]{2,1,0:T(8,128)S(1)} %get-tuple-element.28.last, ...), custom_call_target="tpu_custom_call", output_to_operand_aliasing={{0}: (4, {}), {1}: (5, {})} | custom-call | tf_op jit(solution)/shard_map/after/pallas_call | solution.py:295
Async XLA Ops:
  1.7 7.4 %collective-permute-start = (f32[33,4,256]{2,1,0:T(4,128)S(1)}, f32[33,4,256]{2,1,0:T(4,128)S(1)}, u32[]{:S(2)}, u32[]{:S(2)}) collective-permute-start(f32[33,4,256]{2,1,0:T(4,128)S(1)} %get-tuple-element.21), channel_id=1, source_target_pairs={{0,2},{2,4},{4,6},{6,8},{8,10},{10,12},{12,14},{14,0},{1,3},{3,5},... | collective-permute-start | bytes 405512 | tf_op jit(solution)/shard_map/ppermute | solution.py:287
  2.2 6.8 %collective-permute-start.1 = (f32[33,4,256]{2,1,0:T(4,128)S(1)}, f32[33,4,256]{2,1,0:T(4,128)S(1)}, u32[]{:S(2)}, u32[]{:S(2)}) collective-permute-start(f32[33,4,256]{2,1,0:T(4,128)S(1)} %get-tuple-element.22.after), channel_id=1, source_target_pairs={{0,14},{2,0},{4,2},{6,4},{8,6},{10,8},{12,10},{14,12},{1,15},{3,1}... | collective-permute-start | bytes 405512 | tf_op jit(solution)/shard_map/ppermute | solution.py:287
  9.5 5.5 %collective-permute-start.2 = (f32[2,56,128]{2,1,0:T(8,128)S(1)}, f32[2,56,128]{2,1,0:T(8,128)S(1)}, u32[]{:S(2)}, u32[]{:S(2)}) collective-permute-start(f32[2,56,128]{2,1,0:T(8,128)S(1)} %get-tuple-element.29), channel_id=1, source_target_pairs={{0,1},{1,0},{2,3},{3,2},{4,5},{5,4},{6,7},{7,6},{8,9},{9,8},{10,11... | collective-permute-start | bytes 172040 | tf_op jit(solution)/shard_map/ppermute | solution.py:287

commit v5 on v4

--- a/solution.py
+++ b/solution.py
@@ -25,8 +25,10 @@
     copies = []
     for k, (out, first) in enumerate(((top, 0), (bot, rows - RIM_R))):
         place = pl.ds(first, RIM_R)
-        copies.append(pltpu.make_async_copy(vec.at[:, place, :], out.at[pl.ds(0, vecs)], sem.at[k, 0]))
-        copies.append(pltpu.make_async_copy(dis.at[place, :], out.at[vecs], sem.at[k, 1]))
+        for part in range(4):
+            some = pl.ds(part * vecs // 4, vecs // 4)
+            copies.append(pltpu.make_async_copy(vec.at[some, place, :], out.at[some], sem.at[k, part]))
+        copies.append(pltpu.make_async_copy(dis.at[place, :], out.at[vecs], sem.at[k, 4]))
     for copy in copies:
         copy.start()
     for copy in copies:
@@ -322,7 +324,7 @@
         pltpu.with_memory_space_constraint(vectors, pltpu.HBM),
         pltpu.with_memory_space_constraint(disorder, pltpu.HBM),
     )
-    top, bot = call(pack_kernel, "pack", 2, [HBM, HBM], (rim, rim), [dma((2, 2))], inputs)
+    top, bot = call(pack_kernel, "pack", 2, [HBM, HBM], (rim, rim), [dma((2, 5))], inputs)
     vec, dis = call(
         load_kernel,
         "load",
@@ -335,7 +337,6 @@
     lo = shift(bot, "row", 1)
     hi = shift(top, "row", -1)
     wide = cols + 16
-    wide += (8 - wide) % 32
     tall = shape(depth, wide, LANES)
     field, edges, dis_turned = call(
         turn_kernel,

time: 28 us -> 27.4 us (0.979)
  Pallas kernels: 8.74 us -> 8.08 us
    pallas_call x7, Pallas kernels: 8.74 us -> 8.08 us  [call(): pl.pallas_call(kernel, out_shape=outs, in_specs=ins, out_specs=(VMEM,) *...]
  transfers between devices with their start and end apart: 3 -> 3, of which waited for: 1 -> 1; matrix products, arithmetic and copies ran while one was open for 0% -> 0% of each run, Pallas kernels for 16% -> 14%
where the time goes in v5:
time: 27.4 us; the launch traced here: 27.1 us
  blocking collectives  9.97 us (36%)
  Pallas kernels  8.08 us (29%)
  starting transfers between devices  6.72 us (25%)
  waiting for transfers between devices  1.66 us (6%)
  between operations  0.68 us (2%)
    all_to_all x1, blocking collectives, body(): sums = lax.all_to_all(spread, AXES, 0, 0)  9.97 us
    pallas_call x7, Pallas kernels, call(): pl.pallas_call(kernel, out_shape=outs, in_specs=ins, out_specs=(VMEM,) *...  8.08 us
    ppermute x3, starting transfers between devices, shift(): lax.ppermute(array, axis, [(i, (i + by) % count) for i in range(count)])  6.72 us
    ppermute x3, waiting for transfers between devices, shift(): lax.ppermute(array, axis, [(i, (i + by) % count) for i in range(count)])  1.66 us
  transfers between devices with their start and end apart: 3, of which 1 were waited for; matrix products, arithmetic and copies ran while one was open for 0% of the time, Pallas kernels for 14%

profile of v5, /device:TPU:0, one launch (start us, length us, event | category | flops | bytes accessed | tf_op | source)
XLA Modules:
  0.0 27.1 jit_solution(2979829129856745292)
XLA Ops:
  0.6 1.0 %pack.1 = (f32[33,4,256]{2,1,0:T(4,128)S(1)}, f32[33,4,256]{2,1,0:T(4,128)S(1)}) custom-call(f32[32,16,256]{2,1,0:T(8,128)} %vec.3, f32[16,256]{1,0:T(8,128)} %dis.3), custom_call_target="tpu_custom_call" | custom-call | tf_op jit(solution)/shard_map/pack/pallas_call | solution.py:297
  1.6 0.5 %collective-permute-start = (f32[33,4,256]{2,1,0:T(4,128)S(1)}, f32[33,4,256]{2,1,0:T(4,128)S(1)}, u32[]{:S(2)}, u32[]{:S(2)}) collective-permute-start(f32[33,4,256]{2,1,0:T(4,128)S(1)} %get-tuple-element.21), channel_id=1, source_target_pairs={{0,2},{2,4},{4,6},{6,8},{8,10},{10,12},{12,14},{14,0},{1,3},{3,5},... | collective-permute-start | bytes 405512 | tf_op jit(solution)/shard_map/ppermute | solution.py:289
  2.2 4.1 %collective-permute-start.1 = (f32[33,4,256]{2,1,0:T(4,128)S(1)}, f32[33,4,256]{2,1,0:T(4,128)S(1)}, u32[]{:S(2)}, u32[]{:S(2)}) collective-permute-start(f32[33,4,256]{2,1,0:T(4,128)S(1)} %get-tuple-element.22.after), channel_id=1, source_target_pairs={{0,14},{2,0},{4,2},{6,4},{8,6},{10,8},{12,10},{14,12},{1,15},{3,1}... | collective-permute-start | bytes 405512 | tf_op jit(solution)/shard_map/ppermute | solution.py:289
  6.3 1.1 %load.1 = (f32[32,16,256]{2,1,0:T(8,128)S(1)}, f32[16,256]{1,0:T(8,128)S(1)}) custom-call(f32[33,4,256]{2,1,0:T(4,128)S(1)} %get-tuple-element.22.after, f32[32,16,256]{2,1,0:T(8,128)} %vec.3, f32[16,256]{1,0:T(8,128)} %dis.3), custom_call_target="tpu_custom_call" | custom-call | tf_op jit(solution)/shard_map/load/pallas_call | solution.py:297
  7.3 1.7 %collective-permute-done.lo = f32[33,4,256]{2,1,0:T(4,128)S(1)} collective-permute-done((f32[33,4,256]{2,1,0:T(4,128)S(1)}, f32[33,4,256]{2,1,0:T(4,128)S(1)}, u32[]{:S(2)}, u32[]{:S(2)}) %collective-permute-start) | collective-permute-done | bytes 135200 | tf_op jit(solution)/shard_map/ppermute | solution.py:289
  9.0 0.0 collective-permute-done.1.hi
  9.0 0.4 %turn.1 = (f32[6,272,128]{2,1,0:T(8,128)S(1)}, f32[2,56,128]{2,1,0:T(8,128)S(1)}, f32[256,128]{1,0:T(8,128)S(1)}) custom-call(f32[33,4,256]{2,1,0:T(4,128)S(1)} %collective-permute-done.lo, f32[33,4,256]{2,1,0:T(4,128)S(1)} %collective-permute-done.1.hi, f32[32,16,256]{2,1,0:T(8,128)S(1)} %get-tuple-element.23.vec, f32[16,256]{1,0:T(8,128)S(1)} %get-tuple-element.24.dis), custom_call_target="tpu_custom_call" | custom-call | tf_op jit(solution)/shard_map/turn/pallas_call | solution.py:297
  9.4 2.1 %collective-permute-start.2 = (f32[2,56,128]{2,1,0:T(8,128)S(1)}, f32[2,56,128]{2,1,0:T(8,128)S(1)}, u32[]{:S(2)}, u32[]{:S(2)}) collective-permute-start(f32[2,56,128]{2,1,0:T(8,128)S(1)} %get-tuple-element.29), channel_id=1, source_target_pairs={{0,1},{1,0},{2,3},{3,2},{4,5},{5,4},{6,7},{7,6},{8,9},{9,8},{10,11... | collective-permute-start | bytes 172040 | tf_op jit(solution)/shard_map/ppermute | solution.py:289
  11.5 2.7 %inner.1 = (f32[6,272,128]{2,1,0:T(8,128)S(1)}, f32[6,272,128]{2,1,0:T(8,128)S(1)}, f32[17,8,128]{2,1,0:T(8,128)S(1)}) custom-call(f32[6,272,128]{2,1,0:T(8,128)S(1)} %get-tuple-element.25.field, f32[256,128]{1,0:T(8,128)S(1)} %get-tuple-element.26.dis_turned), custom_call_target="tpu_custom_call" | custom-call | tf_op jit(solution)/shard_map/inner/pallas_call | solution.py:297
  14.3 0.0 collective-permute-done.2.left.right
  14.3 0.7 %edge.1 = (f32[2,2,6,8,128]{4,3,2,1,0:T(8,128)S(1)}, f32[32,1,128]{2,1,0:T(1,128)S(1)}) custom-call(f32[6,272,128]{2,1,0:T(8,128)S(1)} %get-tuple-element.25.field, f32[256,128]{1,0:T(8,128)S(1)} %get-tuple-element.26.dis_turned, f32[2,56,128]{2,1,0:T(8,128)S(1)} %collective-permute-done.2.left.right, f32[2,56,128]{2,1,0:T(8,128)S(1)} %collective-permute-done.2.left.right, ...), custom_call_target="tpu_custom_call" | custom-call | tf_op jit(solution)/shard_map/edge/pallas_call | solution.py:297
  15.0 1.6 %before.1 = (f32[32,16,256]{2,1,0:T(8,128)}, f32[32,16,256]{2,1,0:T(8,128)}, f32[32,1,128]{2,1,0:T(1,128)S(1)}) custom-call(f32[6,272,128]{2,1,0:T(8,128)S(1)} %get-tuple-element.27.prev, f32[6,272,128]{2,1,0:T(8,128)S(1)} %get-tuple-element.28.last, f32[2,2,6,8,128]{4,3,2,1,0:T(8,128)S(1)} %get-tuple-element.31.ends, f32[32,1,128]{2,1,0:T(1,128)S(1)} %get-tuple-element.32.spread), custom_call_target="tpu_custom_call" | custom-call | tf_op jit(solution)/shard_map/before/pallas_call | solution.py:297
  16.6 10.0 %all_to_all.5.sums = f32[32,1,128]{2,1,0:T(1,128)S(1)} all-to-all(f32[32,1,128]{2,1,0:T(1,128)S(1)} %get-tuple-element.33), channel_id=1, replica_groups=mesh['grp'=2,'row'=8,'col'=2] {'grp','row','col'}, dimensions={0} | all-to-all | bytes 32768 | tf_op jit(solution)/shard_map/all_to_all | solution.py:388
  26.6 0.6 %after.1 = (f32[32,16,256]{2,1,0:T(8,128)}, f32[32,16,256]{2,1,0:T(8,128)}, f32[1,17]{1,0:T(1,128)}) custom-call(f32[32,1,128]{2,1,0:T(1,128)S(1)} %all_to_all.5.sums, f32[6,272,128]{2,1,0:T(8,128)S(1)} %get-tuple-element.27.prev, f32[6,272,128]{2,1,0:T(8,128)S(1)} %get-tuple-element.28.last, ...), custom_call_target="tpu_custom_call", output_to_operand_aliasing={{0}: (4, {}), {1}: (5, {})} | custom-call | tf_op jit(solution)/shard_map/after/pallas_call | solution.py:297
Async XLA Ops:
  1.6 7.4 %collective-permute-start = (f32[33,4,256]{2,1,0:T(4,128)S(1)}, f32[33,4,256]{2,1,0:T(4,128)S(1)}, u32[]{:S(2)}, u32[]{:S(2)}) collective-permute-start(f32[33,4,256]{2,1,0:T(4,128)S(1)} %get-tuple-element.21), channel_id=1, source_target_pairs={{0,2},{2,4},{4,6},{6,8},{8,10},{10,12},{12,14},{14,0},{1,3},{3,5},... | collective-permute-start | bytes 405512 | tf_op jit(solution)/shard_map/ppermute | solution.py:289
  2.2 6.8 %collective-permute-start.1 = (f32[33,4,256]{2,1,0:T(4,128)S(1)}, f32[33,4,256]{2,1,0:T(4,128)S(1)}, u32[]{:S(2)}, u32[]{:S(2)}) collective-permute-start(f32[33,4,256]{2,1,0:T(4,128)S(1)} %get-tuple-element.22.after), channel_id=1, source_target_pairs={{0,14},{2,0},{4,2},{6,4},{8,6},{10,8},{12,10},{14,12},{1,15},{3,1}... | collective-permute-start | bytes 405512 | tf_op jit(solution)/shard_map/ppermute | solution.py:289
  9.4 4.8 %collective-permute-start.2 = (f32[2,56,128]{2,1,0:T(8,128)S(1)}, f32[2,56,128]{2,1,0:T(8,128)S(1)}, u32[]{:S(2)}, u32[]{:S(2)}) collective-permute-start(f32[2,56,128]{2,1,0:T(8,128)S(1)} %get-tuple-element.29), channel_id=1, source_target_pairs={{0,1},{1,0},{2,3},{3,2},{4,5},{5,4},{6,7},{7,6},{8,9},{9,8},{10,11... | collective-permute-start | bytes 172040 | tf_op jit(solution)/shard_map/ppermute | solution.py:289

commit v6 on v5

--- a/solution.py
+++ b/solution.py
@@ -82,6 +82,8 @@
 
 def spread_rows(tile, m, vecs, depth):
     index = lax.broadcasted_iota(jnp.int32, (8, LANES), 1) // vecs * depth + m
+    if m < 0:
+        index = jnp.maximum(index, 0)
     return jnp.take_along_axis(tile, index, axis=1)
 
 
@@ -171,6 +173,7 @@
 ):
     depth = field.shape[0]
     at = depth * RIM_C
+    around = range(-1, depth + 1)
     for side, rim, rim_at, mine in ((0, left, 0, (0, 1)), (1, right, 2, (cols // 8 - 2, cols // 8 - 1))):
         order = [None, *mine] if rim_at == 0 else [*mine, None]
         for k, t in enumerate(order):
@@ -183,22 +186,20 @@
                     value = rim[places[side], m * RIM_C : (m + 1) * RIM_C, :]
                 else:
                     value = field[m, 8 + 8 * t : 16 + 8 * t, :]
-                start[side, m, 8 + 8 * k : 16 + 8 * k, :] = value
-                ene[side, m, 8 * k : 8 * k + 8, :] = spread_rows(tile, m, vecs, depth)
-
-    def reader(ref):
-        return lambda m, t, by: ref[t[0], m, 8 + 8 * t[1] + by : 16 + 8 * t[1] + by, :]
-
-    def writer(ref):
-        def write(m, t, value):
-            ref[t[0], m, 8 + 8 * t[1] : 16 + 8 * t[1], :] = value
-
-        return write
+                start[side, m + 1, 8 + 8 * k : 16 + 8 * k, :] = value
+                if m == 0:
+                    start[side, depth + 1, 8 + 8 * k : 16 + 8 * k, :] = pltpu.roll(value, LANES - vecs, 1)
+                if m == depth - 1:
+                    start[side, 0, 8 + 8 * k : 16 + 8 * k, :] = pltpu.roll(value, vecs, 1)
+            for m in around:
+                ene[side, m + 1, 8 * k : 8 * k + 8, :] = spread_rows(tile, m, vecs, depth)
 
     middle = ((0, 1), (1, 1))
     every = [(side, k) for side in (0, 1) for k in (0, 1, 2)]
+    odd_line = lax.broadcasted_iota(jnp.int32, (8, LANES), 0) % 2 == 1
     lane = lax.broadcasted_iota(jnp.int32, (8, LANES), 1)
-    total = jnp.zeros((8, LANES), F32)
+    zero = jnp.zeros((8, LANES), F32)
+    total = zero
     first = []
 
     def place(total, k, parts):
@@ -208,22 +209,30 @@
         return total + jnp.where(lane == k, value, 0.0)
 
     for n, (now, then, out) in enumerate(chain(start, odd, even)):
-        sums = fresh(depth)
-        advance(
-            depth,
-            vecs,
-            reader(now),
-            None if then is None else reader(then),
-            writer(out),
-            lambda m, t: ene[t[0], m, 8 * t[1] : 8 * t[1] + 8, :],
-            every if n < STEPS - 1 else middle,
-            middle,
-            sums,
-        )
+        squares, crosses, begin = [zero] * depth, [zero] * depth, [zero] * depth
+        for side, k in every if n < STEPS - 1 else middle:
+            low, high = 8 + 8 * k, 16 + 8 * k
+            here = {m: now[side, m + 1, low:high, :] for m in around}
+            for m in around if n % 2 == 0 else range(depth):
+                above, below = here.get(m - 1, here[m]), here.get(m + 1, here[m])
+                vertical = jnp.where(odd_line, below, above) if m % 2 else jnp.where(odd_line, above, below)
+                near = (now[side, m + 1, low - 1 : high - 1, :] + now[side, m + 1, low + 1 : high + 1, :]) + vertical
+                latest = ene[side, m + 1, 8 * k : 8 * k + 8, :] * here[m] - (2.0 / SCALE) * near
+                latest = 0.5 * latest if then is None else latest - then[side, m + 1, low:high, :]
+                out[side, m + 1, low:high, :] = latest
+                if n % 2 == 1 and n < STEPS - 1 and m == 0:
+                    out[side, depth + 1, low:high, :] = pltpu.roll(latest, LANES - vecs, 1)
+                if n % 2 == 1 and n < STEPS - 1 and m == depth - 1:
+                    out[side, 0, low:high, :] = pltpu.roll(latest, vecs, 1)
+                if (side, k) in middle and 0 <= m < depth:
+                    squares[m] = squares[m] + latest * latest
+                    crosses[m] = crosses[m] + latest * here[m]
+                    if n == 0:
+                        begin[m] = begin[m] + here[m] * here[m]
         if n == 0:
-            total = place(total, 0, sums["0"])
-        total = place(total, 2 * n + 1, sums["r"]) if n < STEPS else total
-        total = place(total, 2 * n + 2, sums["s"])
+            total = place(total, 0, begin)
+        total = place(total, 2 * n + 1, crosses)
+        total = place(total, 2 * n + 2, squares)
     line = lane[:1]
     values = jnp.sum(total, axis=0, keepdims=True)
     base = jnp.where(line % 2 == 0, first[0], first[1])
@@ -232,7 +241,7 @@
     for k, ref in ((0, odd if STEPS % 2 == 0 else even), (1, even if STEPS % 2 == 0 else odd)):
         for side in (0, 1):
             for m in range(depth):
-                ends[k, side, m] = ref[side, m, 16:24, :]
+                ends[k, side, m] = ref[side, m + 1, 16:24, :]
 
 
 def on_first_chip():
@@ -362,14 +371,14 @@
         [pltpu.VMEM((depth, cols + 8, LANES), F32)],
         (field, dis_turned),
     )
-    strip = pltpu.VMEM((2, depth, 40, LANES), F32)
+    strip = pltpu.VMEM((2, depth + 2, 48, LANES), F32)
     ends, spread = call(
         functools.partial(edge_kernel, rows, vecs, cols, places, float(sites)),
         "edge",
         6,
         [VMEM] * 5,
         (shape(2, 2, depth, 8, LANES), shape(world, 1, LANES)),
-        [strip, strip, strip, pltpu.VMEM((2, depth, 24, LANES), F32)],
+        [strip, strip, strip, pltpu.VMEM((2, depth + 2, 24, LANES), F32)],
         (field, dis_turned, left, right, partial),
     )
     fields = ((odd, even) if STEPS % 2 == 0 else (even, odd)) + (ends,)

time: 27.4 us -> 27.3 us (level)
  no operation moved by 1% of the time
where the time goes in v6:
time: 27.3 us; the launch traced here: 27.1 us
  blocking collectives  9.97 us (37%)
  Pallas kernels  8.02 us (29%)
  starting transfers between devices  6.72 us (25%)
  waiting for transfers between devices  1.66 us (6%)
  between operations  0.68 us (2%)
    all_to_all x1, blocking collectives, body(): sums = lax.all_to_all(spread, AXES, 0, 0)  9.97 us
    pallas_call x7, Pallas kernels, call(): pl.pallas_call(kernel, out_shape=outs, in_specs=ins, out_specs=(VMEM,) *...  8.02 us
    ppermute x3, starting transfers between devices, shift(): lax.ppermute(array, axis, [(i, (i + by) % count) for i in range(count)])  6.72 us
    ppermute x3, waiting for transfers between devices, shift(): lax.ppermute(array, axis, [(i, (i + by) % count) for i in range(count)])  1.66 us
  transfers between devices with their start and end apart: 3, of which 1 were waited for; matrix products, arithmetic and copies ran while one was open for 0% of the time, Pallas kernels for 14%

profile of v6, /device:TPU:0, one launch (start us, length us, event | category | flops | bytes accessed | tf_op | source)
XLA Modules:
  0.0 27.1 jit_solution(6469070495986544877)
XLA Ops:
  0.6 1.0 %pack.1 = (f32[33,4,256]{2,1,0:T(4,128)S(1)}, f32[33,4,256]{2,1,0:T(4,128)S(1)}) custom-call(f32[32,16,256]{2,1,0:T(8,128)} %vec.3, f32[16,256]{1,0:T(8,128)} %dis.3), custom_call_target="tpu_custom_call" | custom-call | tf_op jit(solution)/shard_map/pack/pallas_call | solution.py:306
  1.6 0.5 %collective-permute-start = (f32[33,4,256]{2,1,0:T(4,128)S(1)}, f32[33,4,256]{2,1,0:T(4,128)S(1)}, u32[]{:S(2)}, u32[]{:S(2)}) collective-permute-start(f32[33,4,256]{2,1,0:T(4,128)S(1)} %get-tuple-element.21), channel_id=1, source_target_pairs={{0,2},{2,4},{4,6},{6,8},{8,10},{10,12},{12,14},{14,0},{1,3},{3,5},... | collective-permute-start | bytes 405512 | tf_op jit(solution)/shard_map/ppermute | solution.py:298
  2.2 4.1 %collective-permute-start.1 = (f32[33,4,256]{2,1,0:T(4,128)S(1)}, f32[33,4,256]{2,1,0:T(4,128)S(1)}, u32[]{:S(2)}, u32[]{:S(2)}) collective-permute-start(f32[33,4,256]{2,1,0:T(4,128)S(1)} %get-tuple-element.22.after), channel_id=1, source_target_pairs={{0,14},{2,0},{4,2},{6,4},{8,6},{10,8},{12,10},{14,12},{1,15},{3,1}... | collective-permute-start | bytes 405512 | tf_op jit(solution)/shard_map/ppermute | solution.py:298
  6.3 1.1 %load.1 = (f32[32,16,256]{2,1,0:T(8,128)S(1)}, f32[16,256]{1,0:T(8,128)S(1)}) custom-call(f32[33,4,256]{2,1,0:T(4,128)S(1)} %get-tuple-element.22.after, f32[32,16,256]{2,1,0:T(8,128)} %vec.3, f32[16,256]{1,0:T(8,128)} %dis.3), custom_call_target="tpu_custom_call" | custom-call | tf_op jit(solution)/shard_map/load/pallas_call | solution.py:306
  7.3 1.7 %collective-permute-done.lo = f32[33,4,256]{2,1,0:T(4,128)S(1)} collective-permute-done((f32[33,4,256]{2,1,0:T(4,128)S(1)}, f32[33,4,256]{2,1,0:T(4,128)S(1)}, u32[]{:S(2)}, u32[]{:S(2)}) %collective-permute-start) | collective-permute-done | bytes 135200 | tf_op jit(solution)/shard_map/ppermute | solution.py:298
  9.0 0.0 collective-permute-done.1.hi
  9.0 0.4 %turn.1 = (f32[6,272,128]{2,1,0:T(8,128)S(1)}, f32[2,56,128]{2,1,0:T(8,128)S(1)}, f32[256,128]{1,0:T(8,128)S(1)}) custom-call(f32[33,4,256]{2,1,0:T(4,128)S(1)} %collective-permute-done.lo, f32[33,4,256]{2,1,0:T(4,128)S(1)} %collective-permute-done.1.hi, f32[32,16,256]{2,1,0:T(8,128)S(1)} %get-tuple-element.23.vec, f32[16,256]{1,0:T(8,128)S(1)} %get-tuple-element.24.dis), custom_call_target="tpu_custom_call" | custom-call | tf_op jit(solution)/shard_map/turn/pallas_call | solution.py:306
  9.4 2.1 %collective-permute-start.2 = (f32[2,56,128]{2,1,0:T(8,128)S(1)}, f32[2,56,128]{2,1,0:T(8,128)S(1)}, u32[]{:S(2)}, u32[]{:S(2)}) collective-permute-start(f32[2,56,128]{2,1,0:T(8,128)S(1)} %get-tuple-element.29), channel_id=1, source_target_pairs={{0,1},{1,0},{2,3},{3,2},{4,5},{5,4},{6,7},{7,6},{8,9},{9,8},{10,11... | collective-permute-start | bytes 172040 | tf_op jit(solution)/shard_map/ppermute | solution.py:298
  11.5 2.7 %inner.1 = (f32[6,272,128]{2,1,0:T(8,128)S(1)}, f32[6,272,128]{2,1,0:T(8,128)S(1)}, f32[17,8,128]{2,1,0:T(8,128)S(1)}) custom-call(f32[6,272,128]{2,1,0:T(8,128)S(1)} %get-tuple-element.25.field, f32[256,128]{1,0:T(8,128)S(1)} %get-tuple-element.26.dis_turned), custom_call_target="tpu_custom_call" | custom-call | tf_op jit(solution)/shard_map/inner/pallas_call | solution.py:306
  14.3 0.0 collective-permute-done.2.left.right
  14.3 0.7 %edge.1 = (f32[2,2,6,8,128]{4,3,2,1,0:T(8,128)S(1)}, f32[32,1,128]{2,1,0:T(1,128)S(1)}) custom-call(f32[6,272,128]{2,1,0:T(8,128)S(1)} %get-tuple-element.25.field, f32[256,128]{1,0:T(8,128)S(1)} %get-tuple-element.26.dis_turned, f32[2,56,128]{2,1,0:T(8,128)S(1)} %collective-permute-done.2.left.right, f32[2,56,128]{2,1,0:T(8,128)S(1)} %collective-permute-done.2.left.right, ...), custom_call_target="tpu_custom_call" | custom-call | tf_op jit(solution)/shard_map/edge/pallas_call | solution.py:306
  15.0 1.6 %before.1 = (f32[32,16,256]{2,1,0:T(8,128)}, f32[32,16,256]{2,1,0:T(8,128)}, f32[32,1,128]{2,1,0:T(1,128)S(1)}) custom-call(f32[6,272,128]{2,1,0:T(8,128)S(1)} %get-tuple-element.27.prev, f32[6,272,128]{2,1,0:T(8,128)S(1)} %get-tuple-element.28.last, f32[2,2,6,8,128]{4,3,2,1,0:T(8,128)S(1)} %get-tuple-element.31.ends, f32[32,1,128]{2,1,0:T(1,128)S(1)} %get-tuple-element.32.spread), custom_call_target="tpu_custom_call" | custom-call | tf_op jit(solution)/shard_map/before/pallas_call | solution.py:306
  16.5 10.0 %all_to_all.5.sums = f32[32,1,128]{2,1,0:T(1,128)S(1)} all-to-all(f32[32,1,128]{2,1,0:T(1,128)S(1)} %get-tuple-element.33), channel_id=1, replica_groups=mesh['grp'=2,'row'=8,'col'=2] {'grp','row','col'}, dimensions={0} | all-to-all | bytes 32768 | tf_op jit(solution)/shard_map/all_to_all | solution.py:397
  26.5 0.6 %after.1 = (f32[32,16,256]{2,1,0:T(8,128)}, f32[32,16,256]{2,1,0:T(8,128)}, f32[1,17]{1,0:T(1,128)}) custom-call(f32[32,1,128]{2,1,0:T(1,128)S(1)} %all_to_all.5.sums, f32[6,272,128]{2,1,0:T(8,128)S(1)} %get-tuple-element.27.prev, f32[6,272,128]{2,1,0:T(8,128)S(1)} %get-tuple-element.28.last, ...), custom_call_target="tpu_custom_call", output_to_operand_aliasing={{0}: (4, {}), {1}: (5, {})} | custom-call | tf_op jit(solution)/shard_map/after/pallas_call | solution.py:306
Async XLA Ops:
  1.6 7.4 %collective-permute-start = (f32[33,4,256]{2,1,0:T(4,128)S(1)}, f32[33,4,256]{2,1,0:T(4,128)S(1)}, u32[]{:S(2)}, u32[]{:S(2)}) collective-permute-start(f32[33,4,256]{2,1,0:T(4,128)S(1)} %get-tuple-element.21), channel_id=1, source_target_pairs={{0,2},{2,4},{4,6},{6,8},{8,10},{10,12},{12,14},{14,0},{1,3},{3,5},... | collective-permute-start | bytes 405512 | tf_op jit(solution)/shard_map/ppermute | solution.py:298
  2.2 6.8 %collective-permute-start.1 = (f32[33,4,256]{2,1,0:T(4,128)S(1)}, f32[33,4,256]{2,1,0:T(4,128)S(1)}, u32[]{:S(2)}, u32[]{:S(2)}) collective-permute-start(f32[33,4,256]{2,1,0:T(4,128)S(1)} %get-tuple-element.22.after), channel_id=1, source_target_pairs={{0,14},{2,0},{4,2},{6,4},{8,6},{10,8},{12,10},{14,12},{1,15},{3,1}... | collective-permute-start | bytes 405512 | tf_op jit(solution)/shard_map/ppermute | solution.py:298
  9.4 4.8 %collective-permute-start.2 = (f32[2,56,128]{2,1,0:T(8,128)S(1)}, f32[2,56,128]{2,1,0:T(8,128)S(1)}, u32[]{:S(2)}, u32[]{:S(2)}) collective-permute-start(f32[2,56,128]{2,1,0:T(8,128)S(1)} %get-tuple-element.29), channel_id=1, source_target_pairs={{0,1},{1,0},{2,3},{3,2},{4,5},{5,4},{6,7},{7,6},{8,9},{9,8},{10,11... | collective-permute-start | bytes 172040 | tf_op jit(solution)/shard_map/ppermute | solution.py:298
